TPU v7x, 128 devices: a whole 4x4x4 slice. The times are simulated.
128 devices in a mesh: blk: 16 (over y, x_hi, core), ulysses: 8 (over x_lo, z).
Axes of the slice: x: 4 (x_hi: 2, x_lo: 2; x = x_hi * 2 + x_lo), y: 4, z: 4, core: 2. Of those that a mesh axis runs over, the one named last changes fastest.
Arguments:
- tokens: bfloat16 [8192, 3072], P(('blk', 'ulysses')), may hold values from -6 to 6
- mod_shift: float32 [3072], replicated, may hold values from -3 to 3
- mod_scale: float32 [3072], replicated, may hold values from -3 to 3
- mod_gate: float32 [3072], replicated, may hold values from 0.5 to 1.5
- qkv_weight: bfloat16 [3, 3072, 3072], P(None, None, 'ulysses'), may hold values from -0.109375 to 0.109375
- query_gain: float32 [128], replicated, may hold values from 1 to 16
- key_gain: float32 [128], replicated, may hold values from 1 to 16
- out_weight: bfloat16 [3072, 3072], P(None, 'ulysses'), may hold values from -0.109375 to 0.109375
Outputs:
- mixed: bfloat16 [8192, 3072], P(('blk', 'ulysses'))
All inputs are finite; a program needn't handle non-finite values.
Results may differ from a plain program's by a relative error of at most 0.013.
The roundings to bfloat16 on the way count: a program that leaves them out, or rounds other values in their place, can miss the bound.
Values may be sent and summed in bfloat16 or wider, within the bound.
A program may use at most 128 MiB of HBM per device.

v0:
```python
import math

import jax
import jax.numpy as jnp
from jax import lax
from jax.sharding import PartitionSpec as P


def head_norm(projected, gain, factor):
    split = projected.reshape(projected.shape[0], -1, gain.shape[0])
    meansq = jnp.mean(split * split, axis=-1, keepdims=True)
    return (split * lax.rsqrt(meansq + 1e-06) * gain * factor).reshape(projected.shape)


def local(tokens, mod_shift, mod_scale, mod_gate, qkv_weight, query_gain, key_gain, out_weight):
    wide = tokens.astype(jnp.float32)
    center = jnp.mean(wide, axis=-1, keepdims=True)
    spread = jnp.mean((wide - center) ** 2, axis=-1, keepdims=True)
    normed = (wide - center) / jnp.sqrt(spread + 1e-06)
    modulated = (normed * (1.0 + mod_scale) + mod_shift).astype(jnp.bfloat16)
    head_size = query_gain.shape[0]
    local_width = qkv_weight.shape[2]
    heads_here = local_width // head_size
    factor = 1.0 / math.sqrt(head_size)
    sums = jnp.einsum(
        "rd,jde->jre",
        lax.all_gather(modulated, "ulysses", axis=0, tiled=True),
        qkv_weight,
        preferred_element_type=jnp.float32,
    )
    queries = head_norm(sums[0], query_gain, factor)
    keys = head_norm(sums[1], key_gain, 1.0)
    stacked = jnp.stack([queries, keys, sums[2]]).astype(jnp.bfloat16)
    queries, keys, values = (stacked[0], stacked[1], stacked[2])
    query_rows = queries.shape[0]
    query_heads = queries.reshape(query_rows, heads_here, head_size)
    start_state = (
        jnp.full((heads_here, query_rows), -1e30, jnp.float32),
        jnp.zeros((heads_here, query_rows), jnp.float32),
        jnp.zeros((heads_here, query_rows, head_size), jnp.float32),
    )
    key_part = lax.all_gather(keys, "blk", axis=0, tiled=True)
    value_part = lax.all_gather(values, "blk", axis=0, tiled=True)
    count = key_part.shape[0] // query_rows

    def step(position, state):
        highest, total, numerator = state
        key_block = lax.dynamic_slice_in_dim(key_part, position * query_rows, query_rows, 0)
        value_block = lax.dynamic_slice_in_dim(value_part, position * query_rows, query_rows, 0)
        key_block = key_block.reshape(query_rows, heads_here, head_size)
        value_block = value_block.reshape(query_rows, heads_here, head_size)
        scores = jnp.einsum(
            "qhd,khd->hqk", query_heads, key_block, preferred_element_type=jnp.float32
        )
        new_high = jnp.maximum(highest, jnp.max(scores, axis=-1))
        rescale = jnp.exp(highest - new_high)
        powers = jnp.exp(scores - new_high[..., None])
        total = total * rescale + jnp.sum(powers, axis=-1)
        numerator = numerator * rescale[..., None] + jnp.einsum(
            "hqk,khd->hqd",
            powers.astype(jnp.bfloat16),
            value_block,
            preferred_element_type=jnp.float32,
        )
        return (new_high, total, numerator)

    highest, total, numerator = lax.fori_loop(0, count, step, start_state)
    attended = (numerator / total[..., None]).transpose(1, 0, 2).reshape(query_rows, local_width)
    attended = attended.astype(jnp.bfloat16)
    columns = jnp.dot(
        lax.all_gather(attended, "ulysses", axis=1, tiled=True),
        out_weight,
        preferred_element_type=jnp.float32,
    )
    branch = lax.all_to_all(
        columns.astype(jnp.bfloat16), "ulysses", split_axis=0, concat_axis=1, tiled=True
    ).astype(columns.dtype)
    return (wide + mod_gate * branch).astype(jnp.bfloat16)


def solution(mesh):
    in_specs = (
        P(("blk", "ulysses"), None),
        P(),
        P(),
        P(),
        P(None, None, "ulysses"),
        P(),
        P(),
        P(None, "ulysses"),
    )
    out_specs = P(("blk", "ulysses"), None)
    return jax.shard_map(local, mesh=mesh, in_specs=in_specs, out_specs=out_specs, check_vma=False)
```

profile of v0, /device:TPU:0, one launch (start us, length us, event | category | flops | bytes accessed | tf_op | source)
XLA Modules:
  0.0 321.3 jit_solution(2371801671310439987)
XLA Ops:
  6.5 1.3 convert_reduce_fusion
  7.9 1.3 fusion.17
  9.9 2.0 fusion.20
  11.9 46.7 %all-gather.7.cloned.1.call-done = bf16[512,3072]{1,0:T(8,128)(2,1)} async-done(((bf16[64,3072]{1,0:T(8,128)(2,1)}), bf16[512,3072]{1,0:T(8,128)(2,1)}) %all-gather.7.cloned.1.call-update) | async-done | bytes 3145744 | tf_op jit(solution)/shard_map/all_gather | solution.py:27
  58.6 7.2 %fusion.12 = f32[3,512,384]{1,2,0:T(8,128)S(1)} fusion(bf16[3,3072,384]{2,1,0:T(8,128)(2,1)} %param.14, bf16[512,3072]{1,0:T(8,128)(2,1)} %all-gather.7.cloned.1.call-done), kind=kOutput, calls=%fused_computation.17 | convolution fusion | flops 3623878656 | bytes 12582912 | tf_op jit(solution)/shard_map/rd,jde->jre/dot_general | solution.py:25
  65.8 1.4 copy-done.2
  68.2 2.5 slice_multiply_fusion
  70.7 1.2 reduce_sum.52
  72.0 2.5 fusion.24
  74.5 1.2 copy.26
  75.8 58.3 %all-gather.13.cloned.1.call-done = bf16[1,8192,384]{1,2,0:T(8,128)(2,1)} async-done(((bf16[1,512,384]{1,2,0:T(8,128)(2,1)}), bf16[1,8192,384]{1,2,0:T(8,128)(2,1)}) %all-gather.13.cloned.1.call-update) | async-done | bytes 6291472 | tf_op jit(solution)/shard_map/all_gather | solution.py:43
  134.1 66.2 %all-gather.11.cloned.1.call-done = bf16[1,8192,384]{1,2,0:T(8,128)(2,1)} async-done(((bf16[1,512,384]{1,2,0:T(8,128)(2,1)}), bf16[1,8192,384]{1,2,0:T(8,128)(2,1)}) %all-gather.11.cloned.1.call-update) | async-done | bytes 6291472 | tf_op jit(solution)/shard_map/all_gather | solution.py:42
  200.3 53.1 %while.18 = (s32[]{:T(128)}, f32[3,512]{1,0:T(4,128)S(1)}, f32[3,512]{1,0:T(4,128)S(1)}, f32[3,512,128]{2,1,0:T(8,128)S(1)}, bf16[8192,384]{0,1:T(8,128)(2,1)}, ...) while((s32[]{:T(128)}, f32[3,512]{1,0:T(4,128)S(1)}, ...), condition=%wide.region_7.0_spmd.clone, body=%wide.region_4.0_spmd.clone.sunk | while | flops 407182848 | bytes 13861043 | solution.py:67
  200.3 1.2 constant_dynamic-slice_fusion.3
  202.6 1.0 fusion.46
  203.6 1.2 constant_dynamic-slice_fusion.3
  205.9 1.0 fusion.46
  206.9 1.2 constant_dynamic-slice_fusion.3
  209.2 1.0 fusion.46
  210.2 1.2 constant_dynamic-slice_fusion.3
  212.5 1.0 fusion.46
  213.5 1.2 constant_dynamic-slice_fusion.3
  215.8 1.0 fusion.46
  216.9 1.2 constant_dynamic-slice_fusion.3
  220.2 1.2 constant_dynamic-slice_fusion.3
  222.5 1.0 fusion.46
  223.5 1.2 constant_dynamic-slice_fusion.3
  225.8 1.0 fusion.46
  226.8 1.2 constant_dynamic-slice_fusion.3
  229.1 1.0 fusion.46
  230.1 1.2 constant_dynamic-slice_fusion.3
  232.4 1.0 fusion.46
  233.5 1.2 constant_dynamic-slice_fusion.3
  235.7 1.0 fusion.46
  236.8 1.2 constant_dynamic-slice_fusion.3
  240.1 1.2 constant_dynamic-slice_fusion.3
  242.4 1.0 fusion.46
  243.4 1.2 constant_dynamic-slice_fusion.3
  245.7 1.0 fusion.46
  246.7 1.2 constant_dynamic-slice_fusion.3
  249.0 1.0 fusion.46
  250.0 1.2 constant_dynamic-slice_fusion.3
  252.3 1.0 fusion.46
  253.3 1.2 copy.27
  254.5 2.0 divide_convert_fusion
  256.5 42.0 %all-gather.9.cloned.1.call-done = bf16[512,3072]{0,1:T(8,128)(2,1)} async-done(((bf16[512,384]{0,1:T(8,128)(2,1)}), bf16[512,3072]{0,1:T(8,128)(2,1)}) %all-gather.9.cloned.1.call-update) | async-done | bytes 3145744 | tf_op jit(solution)/shard_map/all_gather | solution.py:71
  298.5 3.7 %convolution_convert_fusion = bf16[512,384]{1,0:T(8,128)(2,1)S(1)} fusion(bf16[512,3072]{0,1:T(8,128)(2,1)} %all-gather.9.cloned.1.call-done, bf16[3072,384]{1,0:T(8,128)(2,1)S(1)} %copy-done), kind=kOutput, calls=%fused_computation.18 | convolution fusion | flops 1208156160 | bytes 5898240 | tf_op jit(solution)/shard_map/dot_general | solution.py:70
  302.2 11.6 %all_to_all.13 = bf16[8,64,384]{2,1,0:T(8,128)(2,1)S(1)} all-to-all(bf16[8,64,384]{2,1,0:T(8,128)(2,1)S(1)} %bitcast.83), channel_id=1, replica_groups=mesh['blk'=16,'ulysses'=8] {'ulysses'}, dimensions={0} | all-to-all | bytes 786432 | tf_op jit(solution)/shard_map/all_to_all | solution.py:75
  (114 shorter events, 22.4 us)
Async XLA Ops:
  6.5 291.9 %copy-start = (bf16[3072,384]{1,0:T(8,128)(2,1)S(1)}, bf16[3072,384]{1,0:T(8,128)(2,1)}, u32[]{:S(2)}) copy-start(bf16[3072,384]{1,0:T(8,128)(2,1)} %param.17) | copy-start | bytes 7077892
  6.5 52.1 %all-gather.7.cloned.1.call-start = ((), (), s32[]{:S(2)}) async-start(), calls=%async_computation.1 | async-start | bytes 3538944 | tf_op jit(solution)/shard_map/all_gather | solution.py:27
  11.8 56.3 %copy-start.4 = (f32[128]{0:T(128)S(1)}, f32[128]{0:T(128)}, u32[]{:S(2)}) copy-start(f32[128]{0:T(128)} %param.15) | copy-start | bytes 1540
  11.9 56.3 %copy-start.5 = (f32[128]{0:T(128)S(1)}, f32[128]{0:T(128)}, u32[]{:S(2)}) copy-start(f32[128]{0:T(128)} %param.16) | copy-start | bytes 1540
  11.9 122.2 %all-gather.13.cloned.1.call-start = ((), (), s32[]{:S(2)}) async-start(), calls=%async_computation.4 | async-start | bytes 6684672 | tf_op jit(solution)/shard_map/all_gather | solution.py:43
  65.8 1.4 copy-start.2
  68.1 132.2 %all-gather.11.cloned.1.call-start = ((), (), s32[]{:S(2)}) async-start(), calls=%async_computation.3 | async-start | bytes 6684672 | tf_op jit(solution)/shard_map/all_gather | solution.py:42
  74.5 224.0 %all-gather.9.cloned.1.call-start = ((), (), s32[]{:S(2)}) async-start(), calls=%async_computation.2 | async-start | bytes 3538944 | tf_op jit(solution)/shard_map/all_gather | solution.py:71
  302.2 11.8 %copy-start.1 = (bf16[64,3072]{1,0:T(8,128)(2,1)S(1)}, bf16[64,3072]{1,0:T(8,128)(2,1)}, u32[]{:S(2)}) copy-start(bf16[64,3072]{1,0:T(8,128)(2,1)} %param.10) | copy-start | bytes 1179652
  302.2 11.8 %copy-start.3 = (f32[3072]{0:T(1024)S(1)}, f32[3072]{0:T(1024)}, u32[]{:S(2)}) copy-start(f32[3072]{0:T(1024)} %param.13) | copy-start | bytes 36868
Sparse Core Ops, SparseCore 0:
  12.0 46.6 all-gather.6
  68.2 65.8 all-gather.12
  136.4 63.8 all-gather.10
  256.6 41.7 all-gather.8
where the time goes:
time: 322 us; the launch traced here: 321 us
  waiting for transfers between devices  213 us (66%)
  matrix products  36.8 us (11%)
  local copies, waits for them, and re-layouts  23.6 us (7%)
  other arithmetic  21.8 us (7%)
  between operations  13.3 us (4%)
  blocking collectives  11.6 us (4%)
    all_gather x1, waiting for transfers between devices, local(): key_part = lax.all_gather(keys, 'blk', axis=0, tiled=True)  66.2 us
    all_gather x1, waiting for transfers between devices, local(): value_part = lax.all_gather(values, 'blk', axis=0, tiled=True)  58.3 us
    all_gather x1, waiting for transfers between devices, local(): lax.all_gather(modulated, 'ulysses', axis=0, tiled=True)  46.7 us
    all_gather x1, waiting for transfers between devices, local(): lax.all_gather(attended, 'ulysses', axis=1, tiled=True)  42 us
    dynamic_slice x16, local copies, waits for them, and re-layouts, step(): lax.dynamic_slice_in_dim(value_part, position * query_rows, query_rows, 0)  18.8 us
    dot_general x16, matrix products, step(): jnp.einsum('hqk,khd->hqd', powers.astype(jnp.bfloat16), value_block, pref...  15.8 us
    all_to_all x1, blocking collectives, local(): lax.all_to_all(columns.astype(jnp.bfloat16), 'ulysses', split_axis=0, con...  11.6 us
    dot_general x16, matrix products, step(): jnp.einsum('qhd,khd->hqk', query_heads, key_block, preferred_element_type...  10.1 us
  transfers between devices with their start and end apart: 4, of which 4 were waited for; matrix products, arithmetic and copies ran while one was open for 2% of the time, Pallas kernels for 0%

commit v1 on v0

v1 whole, which is shorter than its diff:
```python
import math

import jax
import jax.numpy as jnp
from jax import lax
from jax.experimental import pallas as pl
from jax.experimental.pallas import tpu as pltpu
from jax.sharding import PartitionSpec as P

MESH = pl.DeviceIdType.MESH
F32 = jnp.float32
BF16 = jnp.bfloat16
NT = (((1,), (1,)), ((), ()))


def kernel(
    tokens_ref, shift_ref, scale_ref, gate_ref, qgain_ref, kgain_ref, w_hbm, wo_hbm,
    out_ref,
    w, wo, mod, q, kv, att, outb, drec, m_s, l_s, acc, oacc,
    w_sem, a_ssem, a_rsem, b_ssem, b_rsem, c_ssem, c_rsem, d_ssem, d_rsem,
):
    blk = lax.axis_index("blk")
    u = lax.axis_index("ulysses")
    y, xh, core = blk // 4, (blk // 2) % 2, blk % 2
    xl, z = u // 4, u % 4
    x = xh * 2 + xl

    def device(x_, y_, z_, c_):
        return (y_ * 4 + (x_ // 2) * 2 + c_, (x_ % 2) * 4 + z_)

    zp, zm, z2 = (z + 1) % 4, (z + 3) % 4, (z + 2) % 4
    xp, xm, x2 = (x + 1) % 4, (x + 3) % 4, (x + 2) % 4
    yp, ym = (y + 1) % 4, (y + 3) % 4
    dev_zp, dev_zm = device(x, y, zp, core), device(x, y, zm, core)
    dev_xp, dev_xm = device(xp, y, z, core), device(xm, y, z, core)
    dev_x2 = device(x2, y, z, core)
    dev_yp, dev_ym = device(x, yp, z, core), device(x, ym, z, core)
    dev_core = device(x, y, z, 1 - core)

    w_copies = [
        pltpu.make_async_copy(w_hbm.at[j], w.at[:, pl.ds(j * 384, 384)], w_sem.at[j]) for j in range(3)
    ]
    w_copies.append(pltpu.make_async_copy(wo_hbm, wo, w_sem.at[3]))
    for c_ in w_copies:
        c_.start()

    wide = tokens_ref[...].astype(F32)
    center = jnp.mean(wide, axis=-1, keepdims=True)
    spread = jnp.mean((wide - center) ** 2, axis=-1, keepdims=True)
    normed = (wide - center) / jnp.sqrt(spread + 1e-06)
    modulated = (normed * (1.0 + scale_ref[...]) + shift_ref[...]).astype(BF16)
    mod[z] = modulated[:32]
    mod[12 + z] = modulated[32:]

    barrier = pltpu.get_barrier_semaphore()
    partners = [dev_yp, dev_ym, dev_x2, dev_core]
    for d in range(4):
        zd = (z + d) % 4
        if d:
            partners.append(device(x, y, zd, core))
        partners.append(device(xp, y, zd, core))
        partners.append(device(xm, y, zd, core))
    for p in partners:
        pl.semaphore_signal(barrier, inc=1, device_id=p, device_id_type=MESH)
    pl.semaphore_wait(barrier, len(partners))

    sends = []

    def make(src, dst, ssem, rsem, dev):
        return pltpu.make_async_remote_copy(
            src_ref=src, dst_ref=dst, send_sem=ssem, recv_sem=rsem, device_id=dev, device_id_type=MESH
        )

    def send(src, dst, ssem, rsem, dev):
        c_ = make(src, dst, ssem, rsem, dev)
        c_.start()
        sends.append(c_)

    class Gather:
        def __init__(self, own_a, own_b, from_minus, from_plus, ssem, rsem):
            self.a, self.b, self.fm, self.fp = own_a, own_b, from_minus, from_plus
            self.ssem, self.rsem = ssem, rsem

        def send(self, t, src, dst, dev):
            send(src, dst, self.ssem.at[t], self.rsem.at[t], dev)

        def recv(self, t, dst):
            make(dst, dst, self.ssem.at[t], self.rsem.at[t], dev_zp).wait_recv()

        def start(self):
            self.send(0, self.a(z), self.a(z), dev_zp)
            self.send(2, self.b(z), self.b(z), dev_zm)
            self.send(4, self.a(z), self.fm(z), dev_xp)
            self.send(5, self.b(z), self.fp(z), dev_xm)
            self.send(1, self.b(z), self.b(z), dev_zp)
            self.send(3, self.a(z), self.a(z), dev_zm)

        def wave1(self):
            self.recv(0, self.a(zm))
            self.send(7, self.a(zm), self.fm(zm), dev_xp)
            self.send(6, self.a(zm), self.a(zm), dev_zp)
            self.recv(2, self.b(zp))
            self.send(9, self.b(zp), self.fp(zp), dev_xm)
            self.send(8, self.b(zp), self.b(zp), dev_zm)

        def x_own(self):
            self.recv(4, self.fm(z))
            self.recv(5, self.fp(z))

        def wave2(self):
            self.recv(3, self.a(zp))
            self.send(10, self.a(zp), self.fm(zp), dev_xp)
            self.recv(1, self.b(zm))
            self.send(11, self.b(zm), self.fp(zm), dev_xm)

        def wave3(self):
            self.recv(6, self.a(z2))
            self.send(12, self.a(z2), self.fm(z2), dev_xp)
            self.recv(8, self.b(z2))
            self.send(13, self.b(z2), self.fp(z2), dev_xm)

        def x_near(self):
            self.recv(7, self.fm(zm))
            self.recv(9, self.fp(zp))
            self.recv(10, self.fm(zp))
            self.recv(11, self.fp(zm))

        def x_far(self):
            self.recv(12, self.fm(z2))
            self.recv(13, self.fp(z2))

    factor = 1.0 / math.sqrt(128)

    def head_norm(value, gain):
        meansq = jnp.mean(value * value, axis=-1, keepdims=True)
        return value * lax.rsqrt(meansq + 1e-06) * gain

    def project(g, pieces):
        rows = jnp.concatenate([mod[p] for p in pieces], axis=0)
        sums = jnp.dot(rows, w[...], preferred_element_type=F32)
        for h in range(3):
            qh = (head_norm(sums[:, h * 128:h * 128 + 128], qgain_ref[...]) * factor).astype(BF16)
            for i, p in enumerate(pieces):
                q[h, p] = qh[i * 32:i * 32 + 32]
            kh = head_norm(sums[:, 384 + h * 128:384 + h * 128 + 128], kgain_ref[...])
            kv[h, 0, g, 0] = kh.astype(BF16)
            vh = sums[:, 768 + h * 128:768 + h * 128 + 128]
            kv[h, 0, g, 1] = vh.T.astype(BF16)

    ga = Gather(
        lambda i: mod.at[i], lambda i: mod.at[12 + i], lambda i: mod.at[8 + i], lambda i: mod.at[4 + i],
        a_ssem, a_rsem,
    )
    ga.start()
    for c_ in w_copies:
        c_.wait()
    ga.wave1()
    ga.x_own()
    project(0, [z, 12 + z, 8 + z, 4 + z])
    ga.wave2()
    project(1, [zm, 12 + zm, zp, 12 + zp])
    ga.wave3()
    ga.x_near()
    project(2, [8 + zm, 4 + zm, 8 + zp, 4 + zp])
    ga.x_far()
    project(3, [z2, 12 + z2, 8 + z2, 4 + z2])

    def b_send(h, t, src, dst, dev):
        send(src, dst, b_ssem.at[h, t], b_rsem.at[h, t], dev)

    def b_recv(h, t, dst):
        make(dst, dst, b_ssem.at[h, t], b_rsem.at[h, t], dev_yp).wait_recv()

    lo, hi = pl.ds(0, 2), pl.ds(2, 2)
    for h in range(3):
        own = kv.at[h, 0]
        b_send(h, 2, own, kv.at[h, 4], dev_x2)
        b_send(h, 0, own, kv.at[h, 3], dev_yp)
        b_send(h, 1, own, kv.at[h, 1], dev_ym)
        b_send(h, 3, own, kv.at[h, 8], dev_core)

    def b_event(h, e):
        at = lambda s: kv.at[h, s]
        if e == 0:
            b_recv(h, 0, at(3))
            b_send(h, 4, kv.at[h, 3, lo], kv.at[h, 2, lo], dev_yp)
            b_send(h, 5, at(3), at(11), dev_core)
            b_recv(h, 1, at(1))
            b_send(h, 6, kv.at[h, 1, hi], kv.at[h, 2, hi], dev_ym)
            b_send(h, 7, at(1), at(9), dev_core)
        if e == 1:
            b_recv(h, 2, at(4))
            b_send(h, 8, at(4), at(7), dev_yp)
            b_send(h, 9, at(4), at(5), dev_ym)
            b_send(h, 10, at(4), at(12), dev_core)
        if e == 2:
            b_recv(h, 8, at(7))
            b_send(h, 11, kv.at[h, 7, lo], kv.at[h, 6, lo], dev_yp)
            b_send(h, 12, at(7), at(15), dev_core)
            b_recv(h, 9, at(5))
            b_send(h, 13, kv.at[h, 5, hi], kv.at[h, 6, hi], dev_ym)
            b_send(h, 14, at(5), at(13), dev_core)
        if e == 3:
            b_recv(h, 4, kv.at[h, 2, lo])
            b_recv(h, 6, kv.at[h, 2, hi])
            b_send(h, 15, at(2), at(10), dev_core)
        if e == 4:
            b_recv(h, 11, kv.at[h, 6, lo])
            b_recv(h, 13, kv.at[h, 6, hi])
            b_send(h, 16, at(6), at(14), dev_core)
        if e == 5:
            for t, s in ((3, 8), (5, 11), (7, 9), (10, 12), (12, 15), (14, 13), (15, 10), (16, 14)):
                b_recv(h, t, at(s))

    def attend(h):
        m_s[...] = jnp.full_like(m_s, -1e30)
        l_s[...] = jnp.zeros_like(l_s)
        acc[...] = jnp.zeros_like(acc)

        def body(s, carry):
            keys = jnp.concatenate([kv[h, s, g, 0] for g in range(4)], axis=0)
            vals = jnp.concatenate([kv[h, s, g, 1] for g in range(4)], axis=1)
            for half in range(2):
                cols = pl.ds(half * 256, 256)
                queries = q[h, pl.ds(half * 8, 8)].reshape(256, 128)
                scores = lax.dot_general(keys, queries, NT, preferred_element_type=F32)
                old = m_s[:, cols]
                new = jnp.maximum(old, jnp.max(scores, axis=0, keepdims=True))
                rescale = jnp.exp(old - new)
                powers = jnp.exp(scores - new)
                m_s[:, cols] = new
                l_s[:, cols] = l_s[:, cols] * rescale + jnp.sum(powers, axis=0, keepdims=True)
                acc[:, cols] = acc[:, cols] * rescale + jnp.dot(
                    vals, powers.astype(BF16), preferred_element_type=F32
                )
            return carry

        lax.fori_loop(0, 16, body, 0)
        result = (acc[...] / l_s[...]).T.astype(BF16)
        att[h, 0, z, 0] = result[:256]
        att[h, 0, z, 1] = result[256:]

    gathers = []
    for h in range(3):
        gc = Gather(
            lambda i, h=h: att.at[h, 0, i, 0], lambda i, h=h: att.at[h, 0, i, 1],
            lambda i, h=h: att.at[h, 1, i, 1], lambda i, h=h: att.at[h, 1, i, 0],
            c_ssem.at[h], c_rsem.at[h],
        )
        gathers.append(gc)

    for e in range(6):
        b_event(0, e)
    attend(0)
    gathers[0].start()
    for e in range(6):
        b_event(1, e)
    gathers[0].wave1()
    gathers[0].wave2()
    attend(1)
    gathers[1].start()
    for e in range(6):
        b_event(2, e)
    gathers[0].wave3()
    gathers[1].wave1()
    gathers[1].wave2()
    attend(2)
    gathers[2].start()
    gathers[1].wave3()

    def project_out(h, first):
        def body(i, carry):
            z0 = i
            rows = jnp.concatenate(
                [att[h, c_, z0].reshape(512, 128) for c_ in range(2)], axis=1
            )
            weights = jnp.concatenate([wo[(xl * 4 + z0) * 3 + h], wo[((1 - xl) * 4 + z0) * 3 + h]], axis=0)
            oacc[...] += jnp.dot(rows, weights, preferred_element_type=F32)
            return carry

        lax.fori_loop(0, 4, body, 0)

    oacc[...] = jnp.zeros_like(oacc)
    for h in range(3):
        if h == 2:
            gathers[2].wave1()
            gathers[2].wave2()
            gathers[2].wave3()
        gathers[h].x_own()
        gathers[h].x_near()
        gathers[h].x_far()
        project_out(h, h == 0)

    outb[...] = oacc[...].astype(BF16).reshape(16, 32, 384)
    for d in range(4):
        zd = (z + d) % 4
        if d == 0:
            drec[0, u] = outb[z]
            drec[1, u] = outb[12 + z]
        else:
            dev = device(x, y, zd, core)
            send(outb.at[zd], drec.at[0, u], d_ssem.at[0, d], d_rsem.at[0, d], dev)
            send(outb.at[12 + zd], drec.at[1, u], d_ssem.at[1, d], d_rsem.at[1, d], dev)
        send(outb.at[8 + zd], drec.at[0, u], d_ssem.at[2, d], d_rsem.at[2, d], device(xm, y, zd, core))
        send(outb.at[4 + zd], drec.at[1, u], d_ssem.at[3, d], d_rsem.at[3, d], device(xp, y, zd, core))
    for d in range(4):
        zs = (z + 4 - d) % 4
        for kind in range(4):
            if d == 0 and kind < 2:
                continue
            dst = drec.at[kind % 2, (xl if kind < 2 else 1 - xl) * 4 + zs]
            make(dst, dst, d_ssem.at[kind, d], d_rsem.at[kind, d], dev_zp).wait_recv()
    for v in range(8):
        cols = pl.ds(v * 384, 384)
        branch = jnp.concatenate([drec[0, v], drec[1, v]], axis=0).astype(F32)
        out_ref[:, cols] = (tokens_ref[:, cols].astype(F32) + gate_ref[:, cols] * branch).astype(BF16)

    for c_ in sends:
        c_.wait_send()


def local(tokens, mod_shift, mod_scale, mod_gate, qkv_weight, query_gain, key_gain, out_weight):
    vm = pl.BlockSpec(memory_space=pltpu.VMEM)
    anyspace = pl.BlockSpec(memory_space=pl.ANY)
    dma = pltpu.SemaphoreType.DMA
    return pl.pallas_call(
        kernel,
        out_shape=jax.ShapeDtypeStruct(tokens.shape, BF16),
        in_specs=[vm] * 6 + [anyspace] * 2,
        out_specs=vm,
        scratch_shapes=[
            pltpu.VMEM((3072, 1152), BF16),
            pltpu.VMEM((24, 128, 384), BF16),
            pltpu.VMEM((16, 32, 3072), BF16),
            pltpu.VMEM((3, 16, 32, 128), BF16),
            pltpu.VMEM((3, 16, 4, 2, 128, 128), BF16),
            pltpu.VMEM((3, 2, 4, 2, 256, 128), BF16),
            pltpu.VMEM((16, 32, 384), BF16),
            pltpu.VMEM((2, 8, 32, 384), BF16),
            pltpu.VMEM((1, 512), F32),
            pltpu.VMEM((1, 512), F32),
            pltpu.VMEM((128, 512), F32),
            pltpu.VMEM((512, 384), F32),
            dma((4,)),
            dma((14,)), dma((14,)),
            dma((3, 17)), dma((3, 17)),
            dma((3, 14)), dma((3, 14)),
            dma((4, 4)), dma((4, 4)),
        ],
        compiler_params=pltpu.CompilerParams(
            collective_id=0, has_side_effects=True, vmem_limit_bytes=60 * 1024 * 1024
        ),
        name="joint_attention",
    )(
        tokens, mod_shift.reshape(1, -1), mod_scale.reshape(1, -1), mod_gate.reshape(1, -1),
        query_gain.reshape(1, -1), key_gain.reshape(1, -1), qkv_weight, out_weight.reshape(24, 128, 384),
    )


def solution(mesh):
    in_specs = (
        P(("blk", "ulysses"), None),
        P(),
        P(),
        P(),
        P(None, None, "ulysses"),
        P(),
        P(),
        P(None, "ulysses"),
    )
    out_specs = P(("blk", "ulysses"), None)
    return jax.shard_map(local, mesh=mesh, in_specs=in_specs, out_specs=out_specs, check_vma=False)
```

time: 322 us -> 168 us (0.52)
  waiting for transfers between devices: 213 us -> 0 us
  Pallas kernels: 0 us -> 165 us
  matrix products: 36.8 us -> 0 us
  local copies, waits for them, and re-layouts: 23.6 us -> 1.77 us
  other arithmetic: 21.8 us -> 0 us
  between operations: 13.3 us -> 0.01 us
  blocking collectives: 11.6 us -> 0 us
    all_gather x4 -> x0, waiting for transfers between devices: 213 us -> none  [the longest x1 66.2 us: local(): key_part = lax.all_gather(keys, 'blk', axis=0, tiled=True)]
    pallas_call x0 -> x1, Pallas kernels: none -> 165 us  [local(): pl.pallas_call(kernel, out_shape=jax.ShapeDtypeStruct(tokens.shape, BF16)...]
    dot_general x34 -> x0, matrix products: 36.8 us -> none  [the longest x16 15.8 us: step(): jnp.einsum('hqk,khd->hqd', powers.astype(jnp.bfloat16), value_block, pref...]
    dynamic_slice x16 -> x0, local copies, waits for them, and re-layouts: 18.8 us -> none  [step(): lax.dynamic_slice_in_dim(value_part, position * query_rows, query_rows, 0)]
    all_to_all x1 -> x0, blocking collectives: 11.6 us -> none  [local(): lax.all_to_all(columns.astype(jnp.bfloat16), 'ulysses', split_axis=0, con...]
    reduce_sum x20 -> x0, other arithmetic: 10.8 us -> none  [the longest x16 6.98 us: step(): total = total * rescale + jnp.sum(powers, axis=-1)]
    convert_element_type x3 -> x0, other arithmetic: 4.76 us -> none  [the longest x1 1.96 us: local(): attended = attended.astype(jnp.bfloat16)]
  transfers between devices with their start and end apart: 4 -> 0, of which waited for: 4 -> 0; matrix products, arithmetic and copies ran while one was open for 2% -> 0% of each run, Pallas kernels for 0% -> 0%
where the time goes in v1:
time: 168 us; the launch traced here: 167 us
  Pallas kernels  165 us (98%)
  local copies, waits for them, and re-layouts  1.77 us (1%)
    pallas_call x1, Pallas kernels, local(): pl.pallas_call(kernel, out_shape=jax.ShapeDtypeStruct(tokens.shape, BF16)...  165 us

profile of v1, /device:TPU:0, one launch (start us, length us, event | category | flops | bytes accessed | tf_op | source)
XLA Modules:
  0.0 167.2 jit_solution(13619506771780662082)
XLA Ops:
  0.0 165.4 %joint_attention.1 = bf16[64,3072]{1,0:T(8,128)(2,1)} custom-call(bf16[64,3072]{1,0:T(8,128)(2,1)} %tokens_ref.1, f32[1,3072]{1,0:T(1,128)} %bitcast.7, f32[1,3072]{1,0:T(1,128)} %bitcast.8, f32[1,3072]{1,0:T(1,128)} %bitcast.9, f32[1,128]{1,0:T(1,128)} %bitcast.10, f32[1,128]{1,0:T(1,128)} %bitcast.11, bf16[3,3072,384]{2,1,0:T(8,128)(2,1)} %w_hbm.1, ...), custom_call_target="tpu_custom_call" | custom-call | tf_op jit(solution)/shard_map/joint_attention/pallas_call | solution.py:326
  165.4 1.8 %copy.10 = bf16[64,3072]{1,0:T(8,128)(2,1)} copy(bf16[64,3072]{1,0:T(8,128)(2,1)} %joint_attention.1) | data formatting | bytes 786432

commit v2 on v1

--- a/solution.py
+++ b/solution.py
@@ -16,8 +16,9 @@
 def kernel(
     tokens_ref, shift_ref, scale_ref, gate_ref, qgain_ref, kgain_ref, w_hbm, wo_hbm,
     out_ref,
-    w, wo, mod, q, kv, att, outb, drec, m_s, l_s, acc, oacc,
-    w_sem, a_ssem, a_rsem, b_ssem, b_rsem, c_ssem, c_rsem, d_ssem, d_rsem,
+    w, wo, mod, q, kv, att, outb, drec, m_s, l_s, acc, s_s, osend, orecv, stsend, strecv, oacc,
+    w_sem, a_ssem, a_rsem, o_ssem, o_rsem, f_ssem, f_rsem, q_ssem, q_rsem, e_ssem, e_rsem,
+    c_ssem, c_rsem, d_ssem, d_rsem,
 ):
     blk = lax.axis_index("blk")
     u = lax.axis_index("ulysses")
@@ -64,17 +65,16 @@
         pl.semaphore_signal(barrier, inc=1, device_id=p, device_id_type=MESH)
     pl.semaphore_wait(barrier, len(partners))
 
-    sends = []
-
     def make(src, dst, ssem, rsem, dev):
         return pltpu.make_async_remote_copy(
             src_ref=src, dst_ref=dst, send_sem=ssem, recv_sem=rsem, device_id=dev, device_id_type=MESH
         )
 
     def send(src, dst, ssem, rsem, dev):
-        c_ = make(src, dst, ssem, rsem, dev)
-        c_.start()
-        sends.append(c_)
+        make(src, dst, ssem, rsem, dev).start()
+
+    def sent(src, ssem, rsem):
+        make(src, src, ssem, rsem, dev_zp).wait_send()
 
     class Gather:
         def __init__(self, own_a, own_b, from_minus, from_plus, ssem, rsem):
@@ -141,11 +141,40 @@
         for h in range(3):
             qh = (head_norm(sums[:, h * 128:h * 128 + 128], qgain_ref[...]) * factor).astype(BF16)
             for i, p in enumerate(pieces):
-                q[h, p] = qh[i * 32:i * 32 + 32]
+                q[0, h, p] = qh[i * 32:i * 32 + 32]
             kh = head_norm(sums[:, 384 + h * 128:384 + h * 128 + 128], kgain_ref[...])
             kv[h, 0, g, 0] = kh.astype(BF16)
             vh = sums[:, 768 + h * 128:768 + h * 128 + 128]
             kv[h, 0, g, 1] = vh.T.astype(BF16)
+
+    def o_send(h, g, k):
+        slot, dev = ((3, dev_yp), (1, dev_ym), (4, dev_core))[k]
+        send(kv.at[h, 0, g], kv.at[h, slot, g], o_ssem.at[k, h, g], o_rsem.at[k, h, g], dev)
+
+    def o_recv(h, g, k):
+        dst = kv.at[h, (3, 1, 4)[k], g]
+        make(dst, dst, o_ssem.at[k, h, g], o_rsem.at[k, h, g], dev_yp).wait_recv()
+
+    halves = (pl.ds(0, 2), pl.ds(2, 2))
+
+    def f_send(h, k):
+        src, dst, dev = (
+            (kv.at[h, 3, halves[0]], kv.at[h, 2, halves[0]], dev_yp),
+            (kv.at[h, 1, halves[1]], kv.at[h, 2, halves[1]], dev_ym),
+            (kv.at[h, 3], kv.at[h, 7], dev_core),
+            (kv.at[h, 1], kv.at[h, 5], dev_core),
+            (kv.at[h, 2], kv.at[h, 6], dev_core),
+        )[k]
+        send(src, dst, f_ssem.at[h, k], f_rsem.at[h, k], dev)
+
+    def f_recv(h, k):
+        dst = (kv.at[h, 2, halves[0]], kv.at[h, 2, halves[1]], kv.at[h, 7], kv.at[h, 5], kv.at[h, 6])[k]
+        make(dst, dst, f_ssem.at[h, k], f_rsem.at[h, k], dev_yp).wait_recv()
+
+    def own_block(g):
+        for h in range(3):
+            for k in range(3):
+                o_send(h, g, k)
 
     ga = Gather(
         lambda i: mod.at[i], lambda i: mod.at[12 + i], lambda i: mod.at[8 + i], lambda i: mod.at[4 + i],
@@ -157,86 +186,92 @@
     ga.wave1()
     ga.x_own()
     project(0, [z, 12 + z, 8 + z, 4 + z])
+    own_block(0)
     ga.wave2()
     project(1, [zm, 12 + zm, zp, 12 + zp])
+    own_block(1)
     ga.wave3()
     ga.x_near()
     project(2, [8 + zm, 4 + zm, 8 + zp, 4 + zp])
+    own_block(2)
     ga.x_far()
     project(3, [z2, 12 + z2, 8 + z2, 4 + z2])
-
-    def b_send(h, t, src, dst, dev):
-        send(src, dst, b_ssem.at[h, t], b_rsem.at[h, t], dev)
-
-    def b_recv(h, t, dst):
-        make(dst, dst, b_ssem.at[h, t], b_rsem.at[h, t], dev_yp).wait_recv()
-
-    lo, hi = pl.ds(0, 2), pl.ds(2, 2)
-    for h in range(3):
-        own = kv.at[h, 0]
-        b_send(h, 2, own, kv.at[h, 4], dev_x2)
-        b_send(h, 0, own, kv.at[h, 3], dev_yp)
-        b_send(h, 1, own, kv.at[h, 1], dev_ym)
-        b_send(h, 3, own, kv.at[h, 8], dev_core)
-
-    def b_event(h, e):
-        at = lambda s: kv.at[h, s]
-        if e == 0:
-            b_recv(h, 0, at(3))
-            b_send(h, 4, kv.at[h, 3, lo], kv.at[h, 2, lo], dev_yp)
-            b_send(h, 5, at(3), at(11), dev_core)
-            b_recv(h, 1, at(1))
-            b_send(h, 6, kv.at[h, 1, hi], kv.at[h, 2, hi], dev_ym)
-            b_send(h, 7, at(1), at(9), dev_core)
-        if e == 1:
-            b_recv(h, 2, at(4))
-            b_send(h, 8, at(4), at(7), dev_yp)
-            b_send(h, 9, at(4), at(5), dev_ym)
-            b_send(h, 10, at(4), at(12), dev_core)
-        if e == 2:
-            b_recv(h, 8, at(7))
-            b_send(h, 11, kv.at[h, 7, lo], kv.at[h, 6, lo], dev_yp)
-            b_send(h, 12, at(7), at(15), dev_core)
-            b_recv(h, 9, at(5))
-            b_send(h, 13, kv.at[h, 5, hi], kv.at[h, 6, hi], dev_ym)
-            b_send(h, 14, at(5), at(13), dev_core)
-        if e == 3:
-            b_recv(h, 4, kv.at[h, 2, lo])
-            b_recv(h, 6, kv.at[h, 2, hi])
-            b_send(h, 15, at(2), at(10), dev_core)
-        if e == 4:
-            b_recv(h, 11, kv.at[h, 6, lo])
-            b_recv(h, 13, kv.at[h, 6, hi])
-            b_send(h, 16, at(6), at(14), dev_core)
-        if e == 5:
-            for t, s in ((3, 8), (5, 11), (7, 9), (10, 12), (12, 15), (14, 13), (15, 10), (16, 14)):
-                b_recv(h, t, at(s))
-
-    def attend(h):
-        m_s[...] = jnp.full_like(m_s, -1e30)
-        l_s[...] = jnp.zeros_like(l_s)
-        acc[...] = jnp.zeros_like(acc)
-
-        def body(s, carry):
-            keys = jnp.concatenate([kv[h, s, g, 0] for g in range(4)], axis=0)
-            vals = jnp.concatenate([kv[h, s, g, 1] for g in range(4)], axis=1)
-            for half in range(2):
-                cols = pl.ds(half * 256, 256)
-                queries = q[h, pl.ds(half * 8, 8)].reshape(256, 128)
-                scores = lax.dot_general(keys, queries, NT, preferred_element_type=F32)
-                old = m_s[:, cols]
-                new = jnp.maximum(old, jnp.max(scores, axis=0, keepdims=True))
-                rescale = jnp.exp(old - new)
-                powers = jnp.exp(scores - new)
-                m_s[:, cols] = new
-                l_s[:, cols] = l_s[:, cols] * rescale + jnp.sum(powers, axis=0, keepdims=True)
-                acc[:, cols] = acc[:, cols] * rescale + jnp.dot(
-                    vals, powers.astype(BF16), preferred_element_type=F32
-                )
-            return carry
-
-        lax.fori_loop(0, 16, body, 0)
-        result = (acc[...] / l_s[...]).T.astype(BF16)
+    for h in range(3):
+        o_send(h, 3, 1)
+        o_send(h, 3, 2)
+        send(q.at[0, h], q.at[1, h], q_ssem.at[h], q_rsem.at[h], dev_x2)
+    o_send(0, 3, 0)
+    o_send(1, 3, 0)
+    for h in range(3):
+        o_recv(h, 0, 0)
+        o_recv(h, 1, 0)
+        f_send(h, 0)
+        if h == 0:
+            o_send(2, 3, 0)
+
+    def near_y(h):
+        for g in range(4):
+            o_recv(h, g, 1)
+        f_send(h, 1)
+        f_send(h, 3)
+        for g in (2, 3):
+            o_recv(h, g, 0)
+        f_send(h, 2)
+
+    def far_y(h):
+        f_recv(h, 0)
+        f_recv(h, 1)
+        f_send(h, 4)
+
+    def sibling_near(h):
+        f_recv(h, 2)
+        f_recv(h, 3)
+
+    def queries_in(h):
+        make(q.at[1, h], q.at[1, h], q_ssem.at[h], q_rsem.at[h], dev_x2).wait_recv()
+
+    def step_of(j):
+        r = (j + 4) % 7
+        h = jnp.where(j < 3, j, (j + 4) // 7 - 1)
+        partner = jnp.where((r >= 1) & (r <= 4), 1, 0)
+        dy = jnp.where((r == 4) | (r == 6), 2, jnp.where((r == 3) | (r == 5), 3, jnp.where(r == 1, 0, 1)))
+        return h, jnp.where(j < 3, 0, partner), jnp.where(j < 3, 0, dy)
+
+    def score(h, side, slot, buf):
+        keys = jnp.concatenate([kv[h, slot, g, 0] for g in range(4)], axis=0)
+        s_s[buf] = lax.dot_general(keys, q[side, h].reshape(512, 128), NT, preferred_element_type=F32)
+
+    def soft(h, side, slot, buf):
+        vals = jnp.concatenate([kv[h, slot, g, 1] for g in range(4)], axis=1)
+        i = h * 2 + side
+        scores = s_s[buf]
+        old = m_s[i]
+        new = jnp.maximum(old, jnp.max(scores, axis=0, keepdims=True))
+        rescale = jnp.exp(old - new)
+        powers = jnp.exp(scores - new)
+        m_s[i] = new
+        l_s[i] = l_s[i] * rescale + jnp.sum(powers, axis=0, keepdims=True)
+        acc[i] = acc[i] * rescale + jnp.dot(vals, powers.astype(BF16), preferred_element_type=F32)
+
+    def partner_done(h):
+        i = h * 2 + 1
+        osend[h] = (acc[i] / l_s[i]).astype(BF16)
+        stsend[h, 0:1] = m_s[i]
+        stsend[h, 1:2] = l_s[i]
+        send(osend.at[h], orecv.at[h], e_ssem.at[0, h], e_rsem.at[0, h], dev_x2)
+        send(stsend.at[h], strecv.at[h], e_ssem.at[1, h], e_rsem.at[1, h], dev_x2)
+
+    def combine(h):
+        i = h * 2
+        make(orecv.at[h], orecv.at[h], e_ssem.at[0, h], e_rsem.at[0, h], dev_x2).wait_recv()
+        make(strecv.at[h], strecv.at[h], e_ssem.at[1, h], e_rsem.at[1, h], dev_x2).wait_recv()
+        other_m, other_l = strecv[h, 0:1], strecv[h, 1:2]
+        top = jnp.maximum(m_s[i], other_m)
+        mine = jnp.exp(m_s[i] - top)
+        theirs = jnp.exp(other_m - top) * other_l
+        inverse = 1.0 / (l_s[i] * mine + theirs)
+        result = acc[i] * (mine * inverse) + orecv[h].astype(F32) * (theirs * inverse)
+        result = result.T.astype(BF16)
         att[h, 0, z, 0] = result[:256]
         att[h, 0, z, 1] = result[256:]
 
@@ -249,22 +284,52 @@
         )
         gathers.append(gc)
 
-    for e in range(6):
-        b_event(0, e)
-    attend(0)
-    gathers[0].start()
-    for e in range(6):
-        b_event(1, e)
-    gathers[0].wave1()
-    gathers[0].wave2()
-    attend(1)
-    gathers[1].start()
-    for e in range(6):
-        b_event(2, e)
-    gathers[0].wave3()
+    m_s[...] = jnp.full_like(m_s, -1e30)
+    l_s[...] = jnp.zeros_like(l_s)
+    acc[...] = jnp.zeros_like(acc)
+    for h in range(3):
+        for g in range(4):
+            o_recv(h, g, 2)
+    score(0, 0, 0, 0)
+
+    services = {}
+
+    def service(j, *steps):
+        services.setdefault(j, []).extend(steps)
+
+    service(2, lambda: near_y(0))
+    service(3, lambda: sibling_near(0), lambda: queries_in(0))
+    service(4, lambda: near_y(1))
+    service(6, lambda: far_y(0), lambda: near_y(2))
+    service(7, lambda: f_recv(0, 4))
+    service(8, lambda: partner_done(0))
+    service(10, lambda: sibling_near(1), lambda: queries_in(1), lambda: far_y(1))
+    service(14, lambda: f_recv(1, 4), lambda: combine(0), gathers[0].start)
+    service(15, lambda: partner_done(1), lambda: far_y(2))
+    service(17, lambda: sibling_near(2), lambda: queries_in(2))
+    service(19, gathers[0].wave1, gathers[0].wave2)
+    service(21, lambda: f_recv(2, 4), lambda: combine(1), gathers[1].start)
+    service(22, lambda: partner_done(2), gathers[0].wave3)
+
+    def body(j, carry):
+        for at, steps in services.items():
+            @pl.when(j == at)
+            def _(steps=steps):
+                for step in steps:
+                    step()
+
+        h, side, dy = step_of(j)
+        h_, side_, dy_ = step_of(jnp.minimum(j + 1, 23))
+        score(h, side, dy + 4, 1)
+        soft(h, side, dy, 0)
+        score(h_, side_, dy_, 0)
+        soft(h, side, dy + 4, 1)
+        return carry
+
+    lax.fori_loop(0, 24, body, 0)
     gathers[1].wave1()
     gathers[1].wave2()
-    attend(2)
+    combine(2)
     gathers[2].start()
     gathers[1].wave3()
 
@@ -315,8 +380,22 @@
         branch = jnp.concatenate([drec[0, v], drec[1, v]], axis=0).astype(F32)
         out_ref[:, cols] = (tokens_ref[:, cols].astype(F32) + gate_ref[:, cols] * branch).astype(BF16)
 
-    for c_ in sends:
-        c_.wait_send()
+    for gather in [ga] + gathers:
+        for t in range(14):
+            sent(gather.a(z), gather.ssem.at[t], gather.rsem.at[t])
+    for h in range(3):
+        for k in range(3):
+            for g in range(4):
+                sent(kv.at[h, 0, g], o_ssem.at[k, h, g], o_rsem.at[k, h, g])
+        for k in range(5):
+            sent(kv.at[h, 0, halves[0]] if k < 2 else kv.at[h, 0], f_ssem.at[h, k], f_rsem.at[h, k])
+        sent(q.at[0, h], q_ssem.at[h], q_rsem.at[h])
+        sent(osend.at[h], e_ssem.at[0, h], e_rsem.at[0, h])
+        sent(stsend.at[h], e_ssem.at[1, h], e_rsem.at[1, h])
+    for d in range(4):
+        for kind in range(4):
+            if d or kind > 1:
+                sent(outb.at[0], d_ssem.at[kind, d], d_rsem.at[kind, d])
 
 
 def local(tokens, mod_shift, mod_scale, mod_gate, qkv_weight, query_gain, key_gain, out_weight):
@@ -332,18 +411,26 @@
             pltpu.VMEM((3072, 1152), BF16),
             pltpu.VMEM((24, 128, 384), BF16),
             pltpu.VMEM((16, 32, 3072), BF16),
-            pltpu.VMEM((3, 16, 32, 128), BF16),
-            pltpu.VMEM((3, 16, 4, 2, 128, 128), BF16),
+            pltpu.VMEM((2, 3, 16, 32, 128), BF16),
+            pltpu.VMEM((3, 8, 4, 2, 128, 128), BF16),
             pltpu.VMEM((3, 2, 4, 2, 256, 128), BF16),
             pltpu.VMEM((16, 32, 384), BF16),
             pltpu.VMEM((2, 8, 32, 384), BF16),
-            pltpu.VMEM((1, 512), F32),
-            pltpu.VMEM((1, 512), F32),
-            pltpu.VMEM((128, 512), F32),
+            pltpu.VMEM((6, 1, 512), F32),
+            pltpu.VMEM((6, 1, 512), F32),
+            pltpu.VMEM((6, 128, 512), F32),
+            pltpu.VMEM((2, 512, 512), F32),
+            pltpu.VMEM((3, 128, 512), BF16),
+            pltpu.VMEM((3, 128, 512), BF16),
+            pltpu.VMEM((3, 8, 512), F32),
+            pltpu.VMEM((3, 8, 512), F32),
             pltpu.VMEM((512, 384), F32),
             dma((4,)),
             dma((14,)), dma((14,)),
-            dma((3, 17)), dma((3, 17)),
+            dma((3, 3, 4)), dma((3, 3, 4)),
+            dma((3, 5)), dma((3, 5)),
+            dma((3,)), dma((3,)),
+            dma((2, 3)), dma((2, 3)),
             dma((3, 14)), dma((3, 14)),
             dma((4, 4)), dma((4, 4)),
         ],

time: 168 us -> 91.2 us (0.54)
  Pallas kernels: 165 us -> 89.3 us
    pallas_call x1, Pallas kernels: 165 us -> 89.3 us  [local(): pl.pallas_call(kernel, out_shape=jax.ShapeDtypeStruct(tokens.shape, BF16)...]
where the time goes in v2:
time: 91.2 us; the launch traced here: 91.1 us
  Pallas kernels  89.3 us (98%)
  local copies, waits for them, and re-layouts  1.77 us (2%)
    pallas_call x1, Pallas kernels, local(): pl.pallas_call(kernel, out_shape=jax.ShapeDtypeStruct(tokens.shape, BF16)...  89.3 us

profile of v2, /device:TPU:0, one launch (start us, length us, event | category | flops | bytes accessed | tf_op | source)
XLA Modules:
  0.0 91.1 jit_solution(14170008503957282752)
XLA Ops:
  0.0 89.3 %joint_attention.1 = bf16[64,3072]{1,0:T(8,128)(2,1)} custom-call(bf16[64,3072]{1,0:T(8,128)(2,1)} %tokens_ref.1, f32[1,3072]{1,0:T(1,128)} %bitcast.7, f32[1,3072]{1,0:T(1,128)} %bitcast.8, f32[1,3072]{1,0:T(1,128)} %bitcast.9, f32[1,128]{1,0:T(1,128)} %bitcast.10, f32[1,128]{1,0:T(1,128)} %bitcast.11, bf16[3,3072,384]{2,1,0:T(8,128)(2,1)} %w_hbm.1, ...), custom_call_target="tpu_custom_call" | custom-call | tf_op jit(solution)/shard_map/joint_attention/pallas_call | solution.py:405
  89.3 1.8 %copy.10 = bf16[64,3072]{1,0:T(8,128)(2,1)} copy(bf16[64,3072]{1,0:T(8,128)(2,1)} %joint_attention.1) | data formatting | bytes 786432

commit v3 on v2

v3 whole, which is shorter than its diff:
```python
import math

import jax
import jax.numpy as jnp
from jax import lax
from jax.experimental import pallas as pl
from jax.experimental.pallas import tpu as pltpu
from jax.sharding import PartitionSpec as P

MESH = pl.DeviceIdType.MESH
F32 = jnp.float32
BF16 = jnp.bfloat16
LOG2E = math.log2(math.e)


def kernel(
    tokens_ref, shift_ref, scale_ref, gate_ref, qgain_ref, kgain_ref, w_hbm, wo_hbm,
    out_ref,
    w, wo, mod, q, kv, att, outb, drec, m_s, l_s, acc, s_s, qt, osend, orecv, stsend, strecv, oacc,
    w_sem, s_sem, a_rsem, ob_rsem, f_rsem, q_rsem, e_rsem, c_rsem, d_rsem,
):
    blk = lax.axis_index("blk")
    u = lax.axis_index("ulysses")
    y, xh, core = blk // 4, (blk // 2) % 2, blk % 2
    xl, z = u // 4, u % 4
    x = xh * 2 + xl

    def device(x_, y_, z_, c_):
        return (y_ * 4 + (x_ // 2) * 2 + c_, (x_ % 2) * 4 + z_)

    zp, zm, z2 = (z + 1) % 4, (z + 3) % 4, (z + 2) % 4
    xp, xm, x2 = (x + 1) % 4, (x + 3) % 4, (x + 2) % 4
    yp, ym = (y + 1) % 4, (y + 3) % 4
    dev_zp, dev_zm = device(x, y, zp, core), device(x, y, zm, core)
    dev_xp, dev_xm = device(xp, y, z, core), device(xm, y, z, core)
    dev_x2 = device(x2, y, z, core)
    dev_z2 = device(x, y, z2, core)
    dev_yp, dev_ym = device(x, yp, z, core), device(x, ym, z, core)
    dev_core = device(x, y, z, 1 - core)

    barrier = pltpu.get_barrier_semaphore()
    partners = [dev_yp, dev_ym, dev_x2, dev_core]
    for d in range(4):
        zd = (z + d) % 4
        if d:
            partners.append(device(x, y, zd, core))
        partners.append(device(xp, y, zd, core))
        partners.append(device(xm, y, zd, core))
    for p in partners:
        pl.semaphore_signal(barrier, inc=1, device_id=p, device_id_type=MESH)

    w_copies = [
        pltpu.make_async_copy(w_hbm.at[j], w.at[:, pl.ds(j * 384, 384)], w_sem.at[j]) for j in range(3)
    ]
    w_copies.append(pltpu.make_async_copy(wo_hbm, wo, w_sem.at[3]))
    for c_ in w_copies:
        c_.start()

    wide = tokens_ref[...].astype(F32)
    center = jnp.mean(wide, axis=-1, keepdims=True)
    spread = jnp.mean((wide - center) ** 2, axis=-1, keepdims=True)
    normed = (wide - center) / jnp.sqrt(spread + 1e-06)
    modulated = (normed * (1.0 + scale_ref[...]) + shift_ref[...]).astype(BF16)
    mod[z] = modulated[:32]
    mod[12 + z] = modulated[32:]

    pl.semaphore_wait(barrier, len(partners))

    def make(src, dst, ssem, rsem, dev):
        return pltpu.make_async_remote_copy(
            src_ref=src, dst_ref=dst, send_sem=ssem, recv_sem=rsem, device_id=dev, device_id_type=MESH
        )

    def send(src, dst, ssem, rsem, dev):
        make(src, dst, ssem, rsem, dev).start()

    def arrived(dst, rsem):
        make(dst, dst, s_sem.at[0], rsem, dev_zp).wait_recv()

    class Gather:
        def __init__(self, own_a, own_b, from_minus, from_plus, ssem, rsem, slots=range(24)):
            self.a, self.b, self.fm, self.fp = own_a, own_b, from_minus, from_plus
            self.ssem, self.rsem, self.slots = ssem, rsem, slots

        def send(self, t, src, dst, dev):
            send(src, dst, self.ssem, self.rsem.at[self.slots[t]], dev)

        def recv(self, t, dst):
            arrived(dst, self.rsem.at[self.slots[t]])

        def start_split(self):
            for i in range(2):
                part = pl.ds(i * 16, 16)
                self.send(14 if i else 0, self.a(z).at[part], self.a(z).at[part], dev_zp)
                self.send(15 if i else 2, self.b(z).at[part], self.b(z).at[part], dev_zm)
            self.send(4, self.a(z), self.fm(z), dev_xp)
            self.send(5, self.b(z), self.fp(z), dev_xm)
            for i in range(2):
                part = pl.ds(i * 16, 16)
                self.send(18 if i else 1, self.b(z).at[part], self.b(z).at[part], dev_zp)
                self.send(19 if i else 3, self.a(z).at[part], self.a(z).at[part], dev_zm)

        def wave2_split(self):
            for i in range(2):
                part = pl.ds(i * 16, 16)
                self.recv(19 if i else 3, self.a(zp).at[part])
                self.send(20 if i else 10, self.a(zp).at[part], self.fm(zp).at[part], dev_xp)
                self.recv(18 if i else 1, self.b(zm).at[part])
                self.send(21 if i else 11, self.b(zm).at[part], self.fp(zm).at[part], dev_xm)

        def wave1_split(self):
            for i in range(2):
                part = pl.ds(i * 16, 16)
                self.recv(14 if i else 0, self.a(zm).at[part])
                self.send(16 if i else 7, self.a(zm).at[part], self.fm(zm).at[part], dev_xp)
                self.recv(15 if i else 2, self.b(zp).at[part])
                self.send(17 if i else 9, self.b(zp).at[part], self.fp(zp).at[part], dev_xm)
            self.send(6, self.a(zm), self.a(zm), dev_zp)
            self.send(8, self.b(zp), self.b(zp), dev_zm)

        def x_near_split(self):
            for i in range(2):
                part = pl.ds(i * 16, 16)
                self.recv(16 if i else 7, self.fm(zm).at[part])
                self.recv(17 if i else 9, self.fp(zp).at[part])
                self.recv(20 if i else 10, self.fm(zp).at[part])
                self.recv(21 if i else 11, self.fp(zm).at[part])

        def start(self):
            self.send(0, self.a(z), self.a(z), dev_zp)
            self.send(2, self.b(z), self.b(z), dev_zm)
            self.send(4, self.a(z), self.fm(z), dev_xp)
            self.send(5, self.b(z), self.fp(z), dev_xm)
            self.send(1, self.b(z), self.b(z), dev_zp)
            self.send(3, self.a(z), self.a(z), dev_zm)

        def wave1(self):
            self.recv(0, self.a(zm))
            self.send(7, self.a(zm), self.fm(zm), dev_xp)
            self.send(6, self.a(zm), self.a(zm), dev_zp)
            self.recv(2, self.b(zp))
            self.send(9, self.b(zp), self.fp(zp), dev_xm)
            self.send(8, self.b(zp), self.b(zp), dev_zm)

        def x_own(self):
            self.recv(4, self.fm(z))
            self.recv(5, self.fp(z))

        def wave2(self):
            self.recv(3, self.a(zp))
            self.send(10, self.a(zp), self.fm(zp), dev_xp)
            self.recv(1, self.b(zm))
            self.send(11, self.b(zm), self.fp(zm), dev_xm)

        def wave3(self):
            self.recv(7, self.fm(zm))
            self.send(12, self.fm(zm), self.fm(zm), dev_zp)
            self.recv(9, self.fp(zp))
            self.send(13, self.fp(zp), self.fp(zp), dev_zm)

        def wave3_split(self):
            part = pl.ds(16, 16)
            self.recv(16, self.fm(zm).at[part])
            self.send(22, self.fm(zm).at[part], self.fm(zm).at[part], dev_zp)
            self.recv(17, self.fp(zp).at[part])
            self.send(23, self.fp(zp).at[part], self.fp(zp).at[part], dev_zm)
            part = pl.ds(0, 16)
            self.recv(6, self.a(z2))
            self.send(12, self.a(z2).at[part], self.fm(z2).at[part], dev_xp)
            self.recv(8, self.b(z2))
            self.send(13, self.b(z2).at[part], self.fp(z2).at[part], dev_xm)

        def x_near_split(self):
            for i in range(2):
                part = pl.ds(i * 16, 16)
                if i == 0:
                    self.recv(7, self.fm(zm).at[part])
                    self.recv(9, self.fp(zp).at[part])
                self.recv(20 if i else 10, self.fm(zp).at[part])
                self.recv(21 if i else 11, self.fp(zm).at[part])

        def x_far_split(self):
            for i in range(2):
                part = pl.ds(i * 16, 16)
                self.recv(22 if i else 12, self.fm(z2).at[part])
                self.recv(23 if i else 13, self.fp(z2).at[part])

    factor = 1.0 / math.sqrt(128)

    def head_norm(value, gain):
        meansq = jnp.mean(value * value, axis=-1, keepdims=True)
        return value * lax.rsqrt(meansq + 1e-06) * gain

    def project(g, pieces):
        rows = jnp.concatenate([mod[p] for p in pieces], axis=0)
        sums = jnp.dot(rows, w[...], preferred_element_type=F32)
        for h in range(3):
            qh = (head_norm(sums[:, h * 128:h * 128 + 128], qgain_ref[...]) * factor).astype(BF16)
            for i, p in enumerate(pieces):
                q[0, h, p] = qh[i * 32:i * 32 + 32]
            kh = head_norm(sums[:, 384 + h * 128:384 + h * 128 + 128], kgain_ref[...])
            kv[h, 0, g, 0] = kh.astype(BF16)
            vh = sums[:, 768 + h * 128:768 + h * 128 + 128]
            kv[h, 0, g, 1] = vh.T.astype(BF16)

    def o_send(h, g, k):
        slot, dev = ((3, dev_yp), (1, dev_ym), (4, dev_core))[k]
        sem = (1 + h if g else 0, 4 + h, 7)[k]
        send(kv.at[h, 0, g], kv.at[h, slot, g], s_sem.at[1], ob_rsem.at[sem], dev)

    def f_send(h, k):
        if k < 4:
            src, dst, dev = kv.at[h, 1 if k % 2 else 3, k], kv.at[h, 2, k], dev_ym if k % 2 else dev_yp
        else:
            slot = (3, 1, 2)[k - 4]
            src, dst, dev = kv.at[h, slot], kv.at[h, slot + 4], dev_core
        send(src, dst, s_sem.at[1], f_rsem.at[h, max(k - 3, 0)], dev)

    def f_recv(h, k):
        arrived(kv.at[h, (7, 5, 6)[k - 4]], f_rsem.at[h, k - 3])

    def own_block(g, heads=(0, 1, 2)):
        for h in heads:
            for k in range(3):
                o_send(h, g, k)

    ga = Gather(
        lambda i: mod.at[i], lambda i: mod.at[12 + i], lambda i: mod.at[8 + i], lambda i: mod.at[4 + i],
        s_sem.at[0], a_rsem,
    )
    ga.start_split()
    ga.wave1_split()
    ga.x_own()
    for c_ in w_copies[:3]:
        c_.wait()
    project(0, [z, 12 + z, 8 + z, 4 + z])
    own_block(0)
    ga.wave2_split()
    project(1, [zm, 12 + zm, zp, 12 + zp])
    own_block(1)
    ga.wave3_split()
    ga.x_near_split()
    project(2, [8 + zm, 4 + zm, 8 + zp, 4 + zp])
    arrived(kv.at[:, 3, 0], ob_rsem.at[0])
    f_send(0, 0)
    own_block(2)
    ga.x_far_split()
    project(3, [z2, 12 + z2, 8 + z2, 4 + z2])
    for h in range(3):
        if h < 2:
            o_send(h, 3, 0)
            o_send(h, 3, 1)
        o_send(h, 3, 2)
        send(q.at[0, h], q.at[1, h], s_sem.at[2], q_rsem.at[h], dev_x2)

    def near_y(h):
        if h:
            f_send(h, 0)
        arrived(kv.at[h, 1], ob_rsem.at[4 + h])
        f_send(h, 1)
        f_send(h, 3)
        f_send(h, 5)
        arrived(kv.at[h, 3, pl.ds(1, 3)], ob_rsem.at[1 + h])
        f_send(h, 2)
        f_send(h, 4)

    def far_y(h):
        arrived(kv.at[h, 2], f_rsem.at[h, 0])
        f_send(h, 6)

    def sibling_near(h):
        f_recv(h, 4)
        f_recv(h, 5)

    def queries_in(h):
        arrived(q.at[1, h], q_rsem.at[h])
        split_queries(h, 1)

    own_keys, near_keys, sibling_keys, far_keys = range(4)
    order = [(0, 0, own_keys), (1, 0, own_keys), (2, 0, own_keys), (0, 0, near_keys)]
    order += [(1, 0, near_keys), (0, 1, own_keys), (0, 1, near_keys), (0, 1, sibling_keys)]
    order += [(0, 0, sibling_keys), (1, 0, sibling_keys), (0, 1, far_keys), (0, 0, far_keys)]
    order += [(1, 1, own_keys), (1, 1, near_keys), (1, 1, sibling_keys), (2, 1, own_keys)]
    order += [(1, 1, far_keys), (2, 1, near_keys), (1, 0, far_keys), (2, 1, sibling_keys)]
    order += [(2, 1, far_keys), (2, 0, near_keys), (2, 0, sibling_keys), (2, 0, far_keys)]
    codes = [(h * 2 + side) * 4 + k for h, side, k in order]
    words = [sum(c << (5 * n) for n, c in enumerate(codes[w * 6:w * 6 + 6])) for w in range(4)]

    def step_of(j):
        w = j // 6
        word = jnp.where(w < 2, jnp.where(w < 1, words[0], words[1]), jnp.where(w < 3, words[2], words[3]))
        code = jnp.right_shift(word, 5 * (j % 6)) % 32
        i, k = code // 4, code % 4
        return i // 2, i % 2, k + 3 * (k // 2) - 4 * (k // 3), 4 - k + 5 * (k // 2)

    def split_queries(h, side):
        wide_q = q[side, h].reshape(512, 128).astype(F32) * LOG2E
        high = wide_q.astype(BF16)
        low = (wide_q - high.astype(F32)).astype(BF16)
        qt[h * 2 + side] = jnp.concatenate([high, low], axis=1).T

    def score(h, side, slot, buf):
        keys = jnp.concatenate([kv[h, slot, g, 0] for g in range(4)], axis=0)
        keys = jnp.concatenate([keys, keys], axis=1)
        s_s[buf] = jnp.dot(keys, qt[h * 2 + side], preferred_element_type=F32)

    def soft(h, side, slot, buf):
        vals = jnp.concatenate([kv[h, slot, g, 1] for g in range(4)], axis=1)
        i = h * 2 + side
        scores = s_s[buf]
        old = m_s[i]
        new = jnp.maximum(old, jnp.max(scores, axis=0, keepdims=True))
        rescale = jnp.exp2(old - new)
        powers = jnp.exp2(scores - new)
        m_s[i] = new
        l_s[i] = l_s[i] * rescale + jnp.sum(powers, axis=0, keepdims=True)
        acc[i] = acc[i] * rescale + jnp.dot(vals, powers.astype(BF16), preferred_element_type=F32)

    def partner_done(h):
        i = h * 2 + 1
        osend[h] = (acc[i] / l_s[i]).astype(BF16)
        stsend[h, 0:1] = m_s[i]
        stsend[h, 1:2] = l_s[i]
        send(osend.at[h], orecv.at[h], s_sem.at[3], e_rsem.at[0, h], dev_x2)
        send(stsend.at[h], strecv.at[h], s_sem.at[4], e_rsem.at[1, h], dev_x2)

    def combine(h):
        i = h * 2
        arrived(orecv.at[h], e_rsem.at[0, h])
        arrived(strecv.at[h], e_rsem.at[1, h])
        other_m, other_l = strecv[h, 0:1], strecv[h, 1:2]
        top = jnp.maximum(m_s[i], other_m)
        mine = jnp.exp2(m_s[i] - top)
        theirs = jnp.exp2(other_m - top) * other_l
        inverse = 1.0 / (l_s[i] * mine + theirs)
        result = acc[i] * (mine * inverse) + orecv[h].astype(F32) * (theirs * inverse)
        result = result.T.astype(BF16)
        att[h, 0, z, 0] = result[:256]
        att[h, 0, z, 1] = result[256:]

    gathers = []
    for h in range(3):
        gc = Gather(
            lambda i, h=h: att.at[h, 0, i, 0], lambda i, h=h: att.at[h, 0, i, 1],
            lambda i, h=h: att.at[h, 1, i, 1], lambda i, h=h: att.at[h, 1, i, 0],
            s_sem.at[5], c_rsem.at[h], (0, 1, 2, 3, 6, 6, 6, 4, 6, 5, 6, 6, 6, 6),
        )
        gathers.append(gc)

    for h in range(3):
        split_queries(h, 0)
    m_s[...] = jnp.full_like(m_s, -1e30)
    l_s[...] = jnp.zeros_like(l_s)
    acc[...] = jnp.zeros_like(acc)
    arrived(kv.at[:, 4], ob_rsem.at[7])
    score(0, 0, 0, 0)

    services = {}

    def service(j, *steps):
        services.setdefault(j, []).extend(steps)

    def last_own():
        o_send(2, 3, 0)
        o_send(2, 3, 1)

    service(1, lambda: near_y(0), last_own, lambda: near_y(1))
    service(2, lambda: queries_in(0))
    service(3, lambda: sibling_near(0), lambda: sibling_near(1))
    service(4, lambda: far_y(0))
    service(5, lambda: f_recv(0, 6), lambda: queries_in(1), lambda: near_y(2))
    service(6, lambda: partner_done(0), lambda: queries_in(2))
    service(7, lambda: far_y(1))
    service(8, lambda: f_recv(1, 6), lambda: sibling_near(2))
    service(9, lambda: partner_done(1), lambda: far_y(2))
    service(10, lambda: f_recv(2, 6), lambda: combine(0), gathers[0].start)
    service(11, lambda: partner_done(2))

    def dispatch(i, keys):
        if len(keys) == 1:
            for step in services[keys[0]]:
                step()
            return
        middle = len(keys) // 2
        pl.when(i < keys[middle])(lambda: dispatch(i, keys[:middle]))
        pl.when(i >= keys[middle])(lambda: dispatch(i, keys[middle:]))

    for i in range(12):
        services.setdefault(i, [])

    def body(i, carry):
        dispatch(i, sorted(services))
        j = i * 2
        at = [step_of(j), step_of(j + 1), step_of(jnp.minimum(j + 2, 23))]
        for n in range(2):
            (h, side, even, odd), (h_, side_, even_, _) = at[n], at[n + 1]
            score(h, side, odd, 1)
            soft(h, side, even, 0)
            score(h_, side_, even_, 0)
            soft(h, side, odd, 1)
        return carry

    lax.fori_loop(0, 12, body, 0)

    def gathered(h):
        arrived(att.at[h, 0], c_rsem.at[h, 6])

    def project_out(h):
        rows = jnp.concatenate(
            [att[h, c_, z0].reshape(512, 128) for c_ in range(2) for z0 in range(4)], axis=1
        )
        weights = jnp.concatenate(
            [wo[((xl + c_) % 2 * 4 + z0) * 3 + h] for c_ in range(2) for z0 in range(4)], axis=0
        )
        total = jnp.dot(rows, weights, preferred_element_type=F32)
        oacc[...] = total if h == 0 else oacc[...] + total

    combine(1)
    gathers[1].start()
    gathers[0].wave1()
    gathers[0].wave2()
    w_copies[3].wait()
    combine(2)
    gathers[2].start()
    gathers[1].wave1()
    gathers[0].wave3()
    gathers[1].wave2()
    gathers[2].wave1()
    gathers[1].wave3()
    gathers[2].wave2()
    gathered(0)
    project_out(0)
    gathers[2].wave3()
    gathered(1)
    project_out(1)
    gathered(2)
    project_out(2)

    outb[...] = oacc[...].astype(BF16).reshape(16, 32, 384)
    for d in range(4):
        zd = (z + d) % 4
        if d == 0:
            drec[0, u] = outb[z]
            drec[1, u] = outb[12 + z]
        else:
            dev = device(x, y, zd, core)
            send(outb.at[zd], drec.at[0, u], s_sem.at[6], d_rsem.at[0], dev)
            send(outb.at[12 + zd], drec.at[1, u], s_sem.at[6], d_rsem.at[0], dev)
        send(outb.at[8 + zd], drec.at[0, u], s_sem.at[6], d_rsem.at[0], device(xm, y, zd, core))
        send(outb.at[4 + zd], drec.at[1, u], s_sem.at[6], d_rsem.at[0], device(xp, y, zd, core))
    arrived(outb.at[pl.ds(0, 14)], d_rsem.at[0])
    for v in range(8):
        cols = pl.ds(v * 384, 384)
        branch = jnp.concatenate([drec[0, v], drec[1, v]], axis=0).astype(F32)
        out_ref[:, cols] = (tokens_ref[:, cols].astype(F32) + gate_ref[:, cols] * branch).astype(BF16)

    for n, group in enumerate((
        mod.at[pl.ds(0, 14)], kv.at[:, pl.ds(0, 7)], q.at[0], osend, stsend,
        kv.at[:, pl.ds(0, 7), pl.ds(0, 2)], outb.at[pl.ds(0, 14)],
    )):
        make(group, group, s_sem.at[n], d_rsem.at[0], dev_zp).wait_send()


def local(tokens, mod_shift, mod_scale, mod_gate, qkv_weight, query_gain, key_gain, out_weight):
    vm = pl.BlockSpec(memory_space=pltpu.VMEM)
    anyspace = pl.BlockSpec(memory_space=pl.ANY)
    dma = pltpu.SemaphoreType.DMA
    return pl.pallas_call(
        kernel,
        out_shape=jax.ShapeDtypeStruct(tokens.shape, BF16),
        in_specs=[vm] * 6 + [anyspace] * 2,
        out_specs=vm,
        scratch_shapes=[
            pltpu.VMEM((3072, 1152), BF16),
            pltpu.VMEM((24, 128, 384), BF16),
            pltpu.VMEM((16, 32, 3072), BF16),
            pltpu.VMEM((2, 3, 16, 32, 128), BF16),
            pltpu.VMEM((3, 8, 4, 2, 128, 128), BF16),
            pltpu.VMEM((3, 2, 4, 2, 256, 128), BF16),
            pltpu.VMEM((16, 32, 384), BF16),
            pltpu.VMEM((2, 8, 32, 384), BF16),
            pltpu.VMEM((6, 1, 512), F32),
            pltpu.VMEM((6, 1, 512), F32),
            pltpu.VMEM((6, 128, 512), F32),
            pltpu.VMEM((2, 512, 512), F32),
            pltpu.VMEM((6, 256, 512), BF16),
            pltpu.VMEM((3, 128, 512), BF16),
            pltpu.VMEM((3, 128, 512), BF16),
            pltpu.VMEM((3, 8, 512), F32),
            pltpu.VMEM((3, 8, 512), F32),
            pltpu.VMEM((512, 384), F32),
            dma((4,)),
            dma((7,)),
            dma((24,)),
            dma((8,)),
            dma((3, 4)),
            dma((3,)),
            dma((2, 3)),
            dma((3, 7)),
            dma((1,)),
        ],
        compiler_params=pltpu.CompilerParams(
            collective_id=0, has_side_effects=True, vmem_limit_bytes=60 * 1024 * 1024
        ),
        name="joint_attention",
    )(
        tokens, mod_shift.reshape(1, -1), mod_scale.reshape(1, -1), mod_gate.reshape(1, -1),
        query_gain.reshape(1, -1), key_gain.reshape(1, -1), qkv_weight, out_weight.reshape(24, 128, 384),
    )


def solution(mesh):
    in_specs = (
        P(("blk", "ulysses"), None),
        P(),
        P(),
        P(),
        P(None, None, "ulysses"),
        P(),
        P(),
        P(None, "ulysses"),
    )
    out_specs = P(("blk", "ulysses"), None)
    return jax.shard_map(local, mesh=mesh, in_specs=in_specs, out_specs=out_specs, check_vma=False)
```

time: 91.2 us -> 80.9 us (0.89)
  Pallas kernels: 89.3 us -> 79 us
    pallas_call x1, Pallas kernels: 89.3 us -> 79 us  [local(): pl.pallas_call(kernel, out_shape=jax.ShapeDtypeStruct(tokens.shape, BF16)...]
where the time goes in v3:
time: 80.9 us; the launch traced here: 80.7 us
  Pallas kernels  79 us (98%)
  local copies, waits for them, and re-layouts  1.77 us (2%)
    pallas_call x1, Pallas kernels, local(): pl.pallas_call(kernel, out_shape=jax.ShapeDtypeStruct(tokens.shape, BF16)...  79 us
    unnamed x1, local copies, waits for them, and re-layouts  1.77 us

profile of v3, /device:TPU:0, one launch (start us, length us, event | category | flops | bytes accessed | tf_op | source)
XLA Modules:
  0.0 80.7 jit_solution(5179597655240730912)
XLA Ops:
  0.0 79.0 %joint_attention.1 = bf16[64,3072]{1,0:T(8,128)(2,1)} custom-call(bf16[64,3072]{1,0:T(8,128)(2,1)} %tokens_ref.1, f32[1,3072]{1,0:T(1,128)} %bitcast.7, f32[1,3072]{1,0:T(1,128)} %bitcast.8, f32[1,3072]{1,0:T(1,128)} %bitcast.9, f32[1,128]{1,0:T(1,128)} %bitcast.10, f32[1,128]{1,0:T(1,128)} %bitcast.11, bf16[3,3072,384]{2,1,0:T(8,128)(2,1)} %w_hbm.1, ...), custom_call_target="tpu_custom_call" | custom-call | tf_op jit(solution)/shard_map/joint_attention/pallas_call | solution.py:468
  79.0 1.8 %copy.10 = bf16[64,3072]{1,0:T(8,128)(2,1)} copy(bf16[64,3072]{1,0:T(8,128)(2,1)} %joint_attention.1) | data formatting | bytes 786432

commit v4 on v3

--- a/solution.py
+++ b/solution.py
@@ -14,7 +14,7 @@
 
 
 def kernel(
-    tokens_ref, shift_ref, scale_ref, gate_ref, qgain_ref, kgain_ref, w_hbm, wo_hbm,
+    tokens_ref, shift_ref, scale_ref, qgain_ref, kgain_ref, w_hbm, wo_hbm,
     out_ref,
     w, wo, mod, q, kv, att, outb, drec, m_s, l_s, acc, s_s, qt, osend, orecv, stsend, strecv, oacc,
     w_sem, s_sem, a_rsem, ob_rsem, f_rsem, q_rsem, e_rsem, c_rsem, d_rsem,
@@ -129,10 +129,28 @@
         def start(self):
             self.send(0, self.a(z), self.a(z), dev_zp)
             self.send(2, self.b(z), self.b(z), dev_zm)
+            self.send(1, self.b(z), self.b(z), dev_zp)
+            self.send(3, self.a(z), self.a(z), dev_zm)
+
+        def far(self):
+            self.send(6, self.a(z), self.a(z), dev_z2)
+            self.send(8, self.b(z), self.b(z), dev_z2)
+
+        def near(self):
+            self.recv(0, self.a(zm))
+            self.send(7, self.a(zm), self.fm(zm), dev_xp)
+            self.recv(2, self.b(zp))
+            self.send(9, self.b(zp), self.fp(zp), dev_xm)
+
+        def cross(self):
             self.send(4, self.a(z), self.fm(z), dev_xp)
             self.send(5, self.b(z), self.fp(z), dev_xm)
-            self.send(1, self.b(z), self.b(z), dev_zp)
-            self.send(3, self.a(z), self.a(z), dev_zm)
+
+        def wave3_x(self):
+            self.recv(6, self.a(z2))
+            self.send(12, self.a(z2), self.fm(z2), dev_xp)
+            self.recv(8, self.b(z2))
+            self.send(13, self.b(z2), self.fp(z2), dev_xm)
 
         def wave1(self):
             self.recv(0, self.a(zm))
@@ -247,10 +265,11 @@
     ga.x_far_split()
     project(3, [z2, 12 + z2, 8 + z2, 4 + z2])
     for h in range(3):
+        o_send(h, 3, 2)
+    for h in range(3):
         if h < 2:
             o_send(h, 3, 0)
             o_send(h, 3, 1)
-        o_send(h, 3, 2)
         send(q.at[0, h], q.at[1, h], s_sem.at[2], q_rsem.at[h], dev_x2)
 
     def near_y(h):
@@ -280,9 +299,9 @@
     order = [(0, 0, own_keys), (1, 0, own_keys), (2, 0, own_keys), (0, 0, near_keys)]
     order += [(1, 0, near_keys), (0, 1, own_keys), (0, 1, near_keys), (0, 1, sibling_keys)]
     order += [(0, 0, sibling_keys), (1, 0, sibling_keys), (0, 1, far_keys), (0, 0, far_keys)]
-    order += [(1, 1, own_keys), (1, 1, near_keys), (1, 1, sibling_keys), (2, 1, own_keys)]
-    order += [(1, 1, far_keys), (2, 1, near_keys), (1, 0, far_keys), (2, 1, sibling_keys)]
-    order += [(2, 1, far_keys), (2, 0, near_keys), (2, 0, sibling_keys), (2, 0, far_keys)]
+    order += [(1, 1, own_keys), (1, 1, near_keys), (1, 1, sibling_keys), (1, 1, far_keys)]
+    order += [(2, 1, own_keys), (2, 1, near_keys), (2, 1, sibling_keys), (2, 1, far_keys)]
+    order += [(1, 0, far_keys), (2, 0, near_keys), (2, 0, sibling_keys), (2, 0, far_keys)]
     codes = [(h * 2 + side) * 4 + k for h, side, k in order]
     words = [sum(c << (5 * n) for n, c in enumerate(codes[w * 6:w * 6 + 6])) for w in range(4)]
 
@@ -343,7 +362,8 @@
         gc = Gather(
             lambda i, h=h: att.at[h, 0, i, 0], lambda i, h=h: att.at[h, 0, i, 1],
             lambda i, h=h: att.at[h, 1, i, 1], lambda i, h=h: att.at[h, 1, i, 0],
-            s_sem.at[5], c_rsem.at[h], (0, 1, 2, 3, 6, 6, 6, 4, 6, 5, 6, 6, 6, 6),
+            s_sem.at[5], c_rsem.at[h],
+            (0, 1, 2, 3, 6, 6, 4, 6, 5, 6, 6, 6, 6, 6) if h == 2 else (0, 1, 2, 3, 6, 6, 6, 4, 6, 5, 6, 6, 6, 6),
         )
         gathers.append(gc)
 
@@ -352,8 +372,8 @@
     m_s[...] = jnp.full_like(m_s, -1e30)
     l_s[...] = jnp.zeros_like(l_s)
     acc[...] = jnp.zeros_like(acc)
+    score(0, 0, 0, 0)
     arrived(kv.at[:, 4], ob_rsem.at[7])
-    score(0, 0, 0, 0)
 
     services = {}
 
@@ -369,12 +389,12 @@
     service(3, lambda: sibling_near(0), lambda: sibling_near(1))
     service(4, lambda: far_y(0))
     service(5, lambda: f_recv(0, 6), lambda: queries_in(1), lambda: near_y(2))
-    service(6, lambda: partner_done(0), lambda: queries_in(2))
-    service(7, lambda: far_y(1))
-    service(8, lambda: f_recv(1, 6), lambda: sibling_near(2))
-    service(9, lambda: partner_done(1), lambda: far_y(2))
-    service(10, lambda: f_recv(2, 6), lambda: combine(0), gathers[0].start)
-    service(11, lambda: partner_done(2))
+    service(6, lambda: partner_done(0), lambda: far_y(1))
+    service(7, lambda: f_recv(1, 6), lambda: queries_in(2))
+    service(8, lambda: partner_done(1), lambda: sibling_near(2), lambda: far_y(2))
+    service(9, lambda: f_recv(2, 6), lambda: combine(0), gathers[0].start)
+    service(10, lambda: partner_done(2), gathers[0].cross)
+    service(11, lambda: combine(1), gathers[1].start)
 
     def dispatch(i, keys):
         if len(keys) == 1:
@@ -415,44 +435,43 @@
         total = jnp.dot(rows, weights, preferred_element_type=F32)
         oacc[...] = total if h == 0 else oacc[...] + total
 
-    combine(1)
-    gathers[1].start()
     gathers[0].wave1()
     gathers[0].wave2()
     w_copies[3].wait()
     combine(2)
     gathers[2].start()
+    gathers[2].far()
     gathers[1].wave1()
     gathers[0].wave3()
     gathers[1].wave2()
-    gathers[2].wave1()
+    gathers[1].cross()
+    gathers[2].near()
     gathers[1].wave3()
     gathers[2].wave2()
+    gathers[2].wave3_x()
+    gathers[2].cross()
     gathered(0)
     project_out(0)
-    gathers[2].wave3()
     gathered(1)
     project_out(1)
     gathered(2)
     project_out(2)
 
     outb[...] = oacc[...].astype(BF16).reshape(16, 32, 384)
-    for d in range(4):
+    for d in (2, 1, 3, 0):
         zd = (z + d) % 4
-        if d == 0:
-            drec[0, u] = outb[z]
-            drec[1, u] = outb[12 + z]
-        else:
+        send(outb.at[8 + zd], drec.at[0, u], s_sem.at[6], d_rsem.at[0], device(xm, y, zd, core))
+        send(outb.at[4 + zd], drec.at[1, u], s_sem.at[6], d_rsem.at[0], device(xp, y, zd, core))
+        if d:
             dev = device(x, y, zd, core)
             send(outb.at[zd], drec.at[0, u], s_sem.at[6], d_rsem.at[0], dev)
             send(outb.at[12 + zd], drec.at[1, u], s_sem.at[6], d_rsem.at[0], dev)
-        send(outb.at[8 + zd], drec.at[0, u], s_sem.at[6], d_rsem.at[0], device(xm, y, zd, core))
-        send(outb.at[4 + zd], drec.at[1, u], s_sem.at[6], d_rsem.at[0], device(xp, y, zd, core))
+    drec[0, u] = outb[z]
+    drec[1, u] = outb[12 + z]
     arrived(outb.at[pl.ds(0, 14)], d_rsem.at[0])
     for v in range(8):
         cols = pl.ds(v * 384, 384)
-        branch = jnp.concatenate([drec[0, v], drec[1, v]], axis=0).astype(F32)
-        out_ref[:, cols] = (tokens_ref[:, cols].astype(F32) + gate_ref[:, cols] * branch).astype(BF16)
+        out_ref[:, cols] = jnp.concatenate([drec[0, v], drec[1, v]], axis=0)
 
     for n, group in enumerate((
         mod.at[pl.ds(0, 14)], kv.at[:, pl.ds(0, 7)], q.at[0], osend, stsend,
@@ -465,10 +484,10 @@
     vm = pl.BlockSpec(memory_space=pltpu.VMEM)
     anyspace = pl.BlockSpec(memory_space=pl.ANY)
     dma = pltpu.SemaphoreType.DMA
-    return pl.pallas_call(
+    branch = pl.pallas_call(
         kernel,
-        out_shape=jax.ShapeDtypeStruct(tokens.shape, BF16),
-        in_specs=[vm] * 6 + [anyspace] * 2,
+        out_shape=pltpu.VMEM(tokens.shape, BF16),
+        in_specs=[vm] * 5 + [anyspace] * 2,
         out_specs=vm,
         scratch_shapes=[
             pltpu.VMEM((3072, 1152), BF16),
@@ -504,9 +523,10 @@
         ),
         name="joint_attention",
     )(
-        tokens, mod_shift.reshape(1, -1), mod_scale.reshape(1, -1), mod_gate.reshape(1, -1),
+        tokens, mod_shift.reshape(1, -1), mod_scale.reshape(1, -1),
         query_gain.reshape(1, -1), key_gain.reshape(1, -1), qkv_weight, out_weight.reshape(24, 128, 384),
     )
+    return (tokens.astype(F32) + mod_gate * branch.astype(F32)).astype(BF16)
 
 
 def solution(mesh):

time: 80.9 us -> 77.8 us (0.962)
  Pallas kernels: 79 us -> 76.8 us
  local copies, waits for them, and re-layouts: 1.77 us -> 0.01 us
  other arithmetic: 0 us -> 0.87 us
    pallas_call x1, Pallas kernels: 79 us -> 76.8 us  [local(): pl.pallas_call(kernel, out_shape=pltpu.VMEM(tokens.shape, BF16), in_specs...]
    unnamed x1 -> x4, local copies, waits for them, and re-layouts: 1.77 us -> 0.01 us
    convert_element_type x0 -> x1, other arithmetic: none -> 0.87 us  [local(): return (tokens.astype(F32) + mod_gate * branch.astype(F32)).astype(BF16)]
where the time goes in v4:
time: 77.8 us; the launch traced here: 77.7 us
  Pallas kernels  76.8 us (99%)
  other arithmetic  0.87 us (1%)
    pallas_call x1, Pallas kernels, local(): pl.pallas_call(kernel, out_shape=pltpu.VMEM(tokens.shape, BF16), in_specs...  76.8 us

profile of v4, /device:TPU:0, one launch (start us, length us, event | category | flops | bytes accessed | tf_op | source)
XLA Modules:
  0.0 77.7 jit_solution(30927092474857530)
XLA Ops:
  0.0 0.0 copy-start
  0.0 0.0 copy-start.1
  0.0 76.8 %joint_attention.1 = bf16[64,3072]{1,0:T(8,128)(2,1)S(1)} custom-call(bf16[64,3072]{1,0:T(8,128)(2,1)} %tokens_ref.1, f32[1,3072]{1,0:T(1,128)} %bitcast.6, f32[1,3072]{1,0:T(1,128)} %bitcast.7, f32[1,128]{1,0:T(1,128)} %bitcast.8, f32[1,128]{1,0:T(1,128)} %bitcast.9, bf16[3,3072,384]{2,1,0:T(8,128)(2,1)} %w_hbm.1, bf16[24,128,384]{2,1,0:T(8,128)(2,1)} %bitcast.5), custom_call_target="tpu_custom_call" | custom-call | tf_op jit(solution)/shard_map/joint_attention/pallas_call | solution.py:487
  76.8 0.0 copy-done
  76.8 0.0 copy-done.1
  76.8 0.9 %add_convert_fusion = bf16[64,3072]{1,0:T(8,128)(2,1)} fusion(bf16[64,3072]{1,0:T(8,128)(2,1)S(1)} %joint_attention.1, bf16[64,3072]{1,0:T(8,128)(2,1)S(1)} %copy-done, f32[3072]{0:T(1024)S(1)} %copy-done.1), kind=kLoop, calls=%fused_computation | loop fusion | flops 983040 | bytes 1191936 | tf_op jit(solution)/shard_map/convert_element_type | solution.py:529
Async XLA Ops:
  0.0 76.8 %copy-start = (bf16[64,3072]{1,0:T(8,128)(2,1)S(1)}, bf16[64,3072]{1,0:T(8,128)(2,1)}, u32[]{:S(2)}) copy-start(bf16[64,3072]{1,0:T(8,128)(2,1)} %tokens_ref.1) | copy-start | bytes 1179652
  0.0 76.8 %copy-start.1 = (f32[3072]{0:T(1024)S(1)}, f32[3072]{0:T(1024)}, u32[]{:S(2)}) copy-start(f32[3072]{0:T(1024)} %param.11) | copy-start | bytes 36868

commit v5 on v4

--- a/solution.py
+++ b/solution.py
@@ -259,8 +259,6 @@
     ga.wave3_split()
     ga.x_near_split()
     project(2, [8 + zm, 4 + zm, 8 + zp, 4 + zp])
-    arrived(kv.at[:, 3, 0], ob_rsem.at[0])
-    f_send(0, 0)
     own_block(2)
     ga.x_far_split()
     project(3, [z2, 12 + z2, 8 + z2, 4 + z2])
@@ -271,6 +269,9 @@
             o_send(h, 3, 0)
             o_send(h, 3, 1)
         send(q.at[0, h], q.at[1, h], s_sem.at[2], q_rsem.at[h], dev_x2)
+
+    arrived(kv.at[:, 3, 0], ob_rsem.at[0])
+    f_send(0, 0)
 
     def near_y(h):
         if h:

time: 77.8 us -> 76.6 us (0.985)
  Pallas kernels: 76.8 us -> 75.5 us
    pallas_call x1, Pallas kernels: 76.8 us -> 75.5 us  [local(): pl.pallas_call(kernel, out_shape=pltpu.VMEM(tokens.shape, BF16), in_specs...]
where the time goes in v5:
time: 76.6 us; the launch traced here: 76.4 us
  Pallas kernels  75.5 us (99%)
  other arithmetic  0.87 us (1%)
    pallas_call x1, Pallas kernels, local(): pl.pallas_call(kernel, out_shape=pltpu.VMEM(tokens.shape, BF16), in_specs...  75.5 us

profile of v5, /device:TPU:0, one launch (start us, length us, event | category | flops | bytes accessed | tf_op | source)
XLA Modules:
  0.0 76.4 jit_solution(6943519215167064225)
XLA Ops:
  0.0 0.0 copy-start
  0.0 0.0 copy-start.1
  0.0 75.5 %joint_attention.1 = bf16[64,3072]{1,0:T(8,128)(2,1)S(1)} custom-call(bf16[64,3072]{1,0:T(8,128)(2,1)} %tokens_ref.1, f32[1,3072]{1,0:T(1,128)} %bitcast.6, f32[1,3072]{1,0:T(1,128)} %bitcast.7, f32[1,128]{1,0:T(1,128)} %bitcast.8, f32[1,128]{1,0:T(1,128)} %bitcast.9, bf16[3,3072,384]{2,1,0:T(8,128)(2,1)} %w_hbm.1, bf16[24,128,384]{2,1,0:T(8,128)(2,1)} %bitcast.5), custom_call_target="tpu_custom_call" | custom-call | tf_op jit(solution)/shard_map/joint_attention/pallas_call | solution.py:488
  75.5 0.0 copy-done
  75.6 0.0 copy-done.1
  75.6 0.9 %add_convert_fusion = bf16[64,3072]{1,0:T(8,128)(2,1)} fusion(bf16[64,3072]{1,0:T(8,128)(2,1)S(1)} %joint_attention.1, bf16[64,3072]{1,0:T(8,128)(2,1)S(1)} %copy-done, f32[3072]{0:T(1024)S(1)} %copy-done.1), kind=kLoop, calls=%fused_computation | loop fusion | flops 983040 | bytes 1191936 | tf_op jit(solution)/shard_map/convert_element_type | solution.py:530
Async XLA Ops:
  0.0 75.6 %copy-start = (bf16[64,3072]{1,0:T(8,128)(2,1)S(1)}, bf16[64,3072]{1,0:T(8,128)(2,1)}, u32[]{:S(2)}) copy-start(bf16[64,3072]{1,0:T(8,128)(2,1)} %tokens_ref.1) | copy-start | bytes 1179652
  0.0 75.6 %copy-start.1 = (f32[3072]{0:T(1024)S(1)}, f32[3072]{0:T(1024)}, u32[]{:S(2)}) copy-start(f32[3072]{0:T(1024)} %param.11) | copy-start | bytes 36868

commit v6 on v5

--- a/solution.py
+++ b/solution.py
@@ -209,17 +209,20 @@
         meansq = jnp.mean(value * value, axis=-1, keepdims=True)
         return value * lax.rsqrt(meansq + 1e-06) * gain
 
-    def project(g, pieces):
+    def project(g, pieces, send_keys):
         rows = jnp.concatenate([mod[p] for p in pieces], axis=0)
-        sums = jnp.dot(rows, w[...], preferred_element_type=F32)
+        sums = jnp.dot(rows, w[:, 384:], preferred_element_type=F32)
+        for h in range(3):
+            kh = head_norm(sums[:, h * 128:h * 128 + 128], kgain_ref[...])
+            kv[h, 0, g, 0] = kh.astype(BF16)
+            vh = sums[:, 384 + h * 128:384 + h * 128 + 128]
+            kv[h, 0, g, 1] = vh.T.astype(BF16)
+        send_keys()
+        sums = jnp.dot(rows, w[:, :384], preferred_element_type=F32)
         for h in range(3):
             qh = (head_norm(sums[:, h * 128:h * 128 + 128], qgain_ref[...]) * factor).astype(BF16)
             for i, p in enumerate(pieces):
                 q[0, h, p] = qh[i * 32:i * 32 + 32]
-            kh = head_norm(sums[:, 384 + h * 128:384 + h * 128 + 128], kgain_ref[...])
-            kv[h, 0, g, 0] = kh.astype(BF16)
-            vh = sums[:, 768 + h * 128:768 + h * 128 + 128]
-            kv[h, 0, g, 1] = vh.T.astype(BF16)
 
     def o_send(h, g, k):
         slot, dev = ((3, dev_yp), (1, dev_ym), (4, dev_core))[k]
@@ -251,23 +254,23 @@
     ga.x_own()
     for c_ in w_copies[:3]:
         c_.wait()
-    project(0, [z, 12 + z, 8 + z, 4 + z])
-    own_block(0)
+    project(0, [z, 12 + z, 8 + z, 4 + z], lambda: own_block(0))
     ga.wave2_split()
-    project(1, [zm, 12 + zm, zp, 12 + zp])
-    own_block(1)
+    project(1, [zm, 12 + zm, zp, 12 + zp], lambda: own_block(1))
     ga.wave3_split()
     ga.x_near_split()
-    project(2, [8 + zm, 4 + zm, 8 + zp, 4 + zp])
-    own_block(2)
+    project(2, [8 + zm, 4 + zm, 8 + zp, 4 + zp], lambda: own_block(2))
     ga.x_far_split()
-    project(3, [z2, 12 + z2, 8 + z2, 4 + z2])
-    for h in range(3):
-        o_send(h, 3, 2)
-    for h in range(3):
-        if h < 2:
+
+    def last_block():
+        for h in range(3):
+            o_send(h, 3, 2)
+        for h in range(2):
             o_send(h, 3, 0)
             o_send(h, 3, 1)
+
+    project(3, [z2, 12 + z2, 8 + z2, 4 + z2], last_block)
+    for h in range(3):
         send(q.at[0, h], q.at[1, h], s_sem.at[2], q_rsem.at[h], dev_x2)
 
     arrived(kv.at[:, 3, 0], ob_rsem.at[0])

time: 76.6 us -> 76.3 us (level)
  no operation moved by 1% of the time
where the time goes in v6:
time: 76.3 us; the launch traced here: 76.2 us
  Pallas kernels  75.3 us (99%)
  other arithmetic  0.87 us (1%)
    pallas_call x1, Pallas kernels, local(): pl.pallas_call(kernel, out_shape=pltpu.VMEM(tokens.shape, BF16), in_specs...  75.3 us

profile of v6, /device:TPU:0, one launch (start us, length us, event | category | flops | bytes accessed | tf_op | source)
XLA Modules:
  0.0 76.2 jit_solution(14830899906334449163)
XLA Ops:
  0.0 0.0 copy-start
  0.0 0.0 copy-start.1
  0.0 75.3 %joint_attention.1 = bf16[64,3072]{1,0:T(8,128)(2,1)S(1)} custom-call(bf16[64,3072]{1,0:T(8,128)(2,1)} %tokens_ref.1, f32[1,3072]{1,0:T(1,128)} %bitcast.6, f32[1,3072]{1,0:T(1,128)} %bitcast.7, f32[1,128]{1,0:T(1,128)} %bitcast.8, f32[1,128]{1,0:T(1,128)} %bitcast.9, bf16[3,3072,384]{2,1,0:T(8,128)(2,1)} %w_hbm.1, bf16[24,128,384]{2,1,0:T(8,128)(2,1)} %bitcast.5), custom_call_target="tpu_custom_call" | custom-call | tf_op jit(solution)/shard_map/joint_attention/pallas_call | solution.py:491
  75.3 0.0 copy-done
  75.3 0.0 copy-done.1
  75.3 0.9 %add_convert_fusion = bf16[64,3072]{1,0:T(8,128)(2,1)} fusion(bf16[64,3072]{1,0:T(8,128)(2,1)S(1)} %joint_attention.1, bf16[64,3072]{1,0:T(8,128)(2,1)S(1)} %copy-done, f32[3072]{0:T(1024)S(1)} %copy-done.1), kind=kLoop, calls=%fused_computation | loop fusion | flops 983040 | bytes 1191936 | tf_op jit(solution)/shard_map/convert_element_type | solution.py:533
Async XLA Ops:
  0.0 75.3 %copy-start = (bf16[64,3072]{1,0:T(8,128)(2,1)S(1)}, bf16[64,3072]{1,0:T(8,128)(2,1)}, u32[]{:S(2)}) copy-start(bf16[64,3072]{1,0:T(8,128)(2,1)} %tokens_ref.1) | copy-start | bytes 1179652
  0.0 75.3 %copy-start.1 = (f32[3072]{0:T(1024)S(1)}, f32[3072]{0:T(1024)}, u32[]{:S(2)}) copy-start(f32[3072]{0:T(1024)} %param.11) | copy-start | bytes 36868
